TPU v7x, 128 devices: a whole 4x4x4 slice. The times are simulated.
128 devices in a mesh: bank: 4 (over x_hi, core), lane: 32 (over z, y, x_lo).
Axes of the slice: x: 4 (x_hi: 2, x_lo: 2; x = x_hi * 2 + x_lo), y: 4, z: 4, core: 2. Of those that a mesh axis runs over, the one named last changes fastest.
Arguments:
- amplitudes: float32 [2, 1024, 128, 128], P(None, ('bank', 'lane')), may hold values from -6 to 6
- energies: float32 [1024, 128, 128], P(('bank', 'lane')), may hold values from -2 to 2
- diagonal_angles: float32 [2, 128], replicated, may hold values from 0.3 to 1.2
Outputs:
- final_parts: float32 [2, 1024, 128, 128], P(None, ('bank', 'lane'))
- marginal: float32 [256, 128, 128], P('lane', 'bank')
All inputs are finite; a program needn't handle non-finite values.
Results may differ from a plain program's by a relative error of at most 0.0003.
Values sent between devices are 32-bit elements; how exact they have to be, the bound alone decides.
No kernel may reach another device: no remote copies, remote signals or barrier semaphores. Data moves between devices by JAX's collectives and lax.ppermute only.
A program may use at most 64 MiB of HBM per device.

v0:
```python
import jax
import jax.numpy as jnp
from jax import lax
from jax.sharding import PartitionSpec as P

LAYERS = 2


def cut_along(shard, dim, size):
    shape = shard.shape
    parts = shard.reshape(*shape[:dim], size, shape[dim] // size, *shape[dim + 1 :])
    return jnp.moveaxis(parts, dim, 0)


def sent_and_summed(shard, axis, dim):
    size = lax.axis_size(axis)
    parts = lax.all_to_all(cut_along(shard, dim, size), axis, 0, 0, tiled=True)
    return jnp.sum(parts, axis=0)


def count_bits(values, count):
    places = jnp.arange(count.bit_length() - 1, dtype=jnp.int32)
    return jnp.sum(values[..., None] >> places & 1, axis=-1)


def walsh_table(count):
    rank = jnp.arange(count, dtype=jnp.int32)
    parity = count_bits(rank[:, None] & rank[None, :], count) % 2
    real_part = jnp.where(parity == 1, -1.0, 1.0).astype(jnp.float32) * count ** (-0.5)
    return real_part


def apply_along(values, dim):
    real_part = walsh_table(values.shape[dim])
    moved = jnp.tensordot(values, real_part, axes=([dim], [0]), precision=lax.Precision.HIGHEST)
    return jnp.moveaxis(moved, -1, dim)


def diagonal_step(values, levels, angle):
    turn = angle * levels
    return jnp.stack(
        [
            values[0] * jnp.cos(turn) + values[1] * jnp.sin(turn),
            values[1] * jnp.cos(turn) - values[0] * jnp.sin(turn),
        ]
    )


def shards(amplitudes, energies, diagonal_angles):
    values = amplitudes
    for layer in range(LAYERS):
        values = diagonal_step(values, energies, diagonal_angles[layer])
        values = apply_along(values, 3)
        values = apply_along(values, 2)
        moved = lax.all_to_all(values, "bank", split_axis=2, concat_axis=1, tiled=True)
        moved = apply_along(moved, 1)
        values = lax.all_to_all(moved, "bank", split_axis=1, concat_axis=2, tiled=True)
        moved = lax.all_to_all(values, "lane", split_axis=3, concat_axis=1, tiled=True)
        spread = moved.reshape(2, lax.axis_size("lane"), -1, moved.shape[2], moved.shape[3])
        moved = apply_along(spread, 1).reshape(moved.shape)
        values = lax.all_to_all(moved, "lane", split_axis=1, concat_axis=3, tiled=True)
    chance = values[0] * values[0] + values[1] * values[1]
    marginal = sent_and_summed(chance, "bank", 1) / lax.axis_size("bank")
    return (values, marginal)


def solution(mesh):
    return jax.shard_map(
        shards,
        mesh=mesh,
        in_specs=(P(None, ("bank", "lane"), None, None), P(("bank", "lane"), None, None), P()),
        out_specs=(P(None, ("bank", "lane"), None, None), P("lane", "bank", None)),
        check_vma=False,
    )
```

profile of v0, /device:TPU:1, one launch (start us, length us, event | category | flops | bytes accessed | tf_op | source)
XLA Modules:
  0.0 207.4 jit_solution(16305064443927837955)
XLA Ops:
  0.6 0.8 slice_bitcast_fusion
  1.5 3.1 %fusion.18 = (f32[1,8,128,128]{3,2,1,0:T(8,128)S(1)}, f32[1,8,128,128]{3,2,1,0:T(8,128)S(1)}) fusion(f32[2,8,128,128]{3,2,1,0:T(8,128)} %param.3, f32[8,128,128]{2,1,0:T(8,128)} %param.4, f32[128]{0:T(128)S(1)} %get-tuple-element.17), kind=kLoop, calls=%fused_computation.32 | loop fusion | flops 917504 | bytes 2621952 | tf_op jit(solution)/shard_map/stack | solution.py:41
  4.6 1.1 fusion
  5.7 1.0 convolution_bitcast_fusion.5
  6.7 1.4 copy.98
  8.0 5.8 %all-to-all-start = ((f32[2,8,128,128]{3,1,0,2:T(8,128)}), f32[2,8,128,128]{3,1,0,2:T(8,128)S(1)}, u32[]{:S(2)}, u32[]{:S(2)}) async-start(f32[2,8,128,128]{3,1,0,2:T(8,128)} %copy.98), calls=%async_computation | async-start | bytes 2097152 | tf_op jit(solution)/shard_map/all_to_all | solution.py:55
  13.9 14.9 %all-to-all-done = f32[2,8,128,128]{3,1,0,2:T(8,128)S(1)} async-done(((f32[2,8,128,128]{3,1,0,2:T(8,128)}), f32[2,8,128,128]{3,1,0,2:T(8,128)S(1)}, u32[]{:S(2)}, u32[]{:S(2)}) %all-to-all-start) | async-done | bytes 1048608 | tf_op jit(solution)/shard_map/all_to_all | solution.py:55
  28.8 1.0 convolution_bitcast_fusion.4
  29.8 0.6 copy.102
  30.4 18.3 %all_to_all.140 = f32[2,32,32,128]{3,2,0,1:T(8,128)S(1)} all-to-all(f32[2,32,32,128]{3,2,0,1:T(8,128)S(1)} %copy.102), channel_id=1, replica_groups=mesh['bank'=4,'lane'=32] {'bank'}, dimensions={1} | all-to-all | bytes 2097152 | tf_op jit(solution)/shard_map/all_to_all | solution.py:57
  49.3 24.5 %all_to_all.141 = f32[2,8,128,128]{2,1,0,3:T(8,128)S(1)} all-to-all(f32[2,8,128,128]{2,1,0,3:T(8,128)S(1)} %copy.105), channel_id=1, replica_groups=mesh['bank'=4,'lane'=32] {'lane'}, dimensions={3} | all-to-all | bytes 2097152 | tf_op jit(solution)/shard_map/all_to_all | solution.py:58
  73.8 1.7 convolution_bitcast_fusion.3
  76.2 0.7 copy.110
  76.8 19.5 %all_to_all.142 = f32[2,256,128,4]{2,3,0,1:T(4,128)S(1)} all-to-all(f32[2,256,128,4]{2,3,0,1:T(4,128)S(1)} %copy.110), channel_id=1, replica_groups=mesh['bank'=4,'lane'=32] {'lane'}, dimensions={1} | all-to-all | bytes 2097152 | tf_op jit(solution)/shard_map/all_to_all | solution.py:61
  97.6 2.0 add_bitcast_fusion
  99.6 1.1 fusion.4
  100.8 1.0 convolution_bitcast_fusion.2
  102.2 20.6 %all_to_all.143 = f32[2,8,128,128]{3,1,0,2:T(8,128)S(1)} all-to-all(f32[2,8,128,128]{3,1,0,2:T(8,128)S(1)} %copy.119), channel_id=1, replica_groups=mesh['bank'=4,'lane'=32] {'bank'}, dimensions={2} | all-to-all | bytes 2097152 | tf_op jit(solution)/shard_map/all_to_all | solution.py:55
  122.8 1.0 convolution_bitcast_fusion.1
  123.8 0.6 copy.123
  124.4 18.4 %all_to_all.144 = f32[2,32,32,128]{3,2,0,1:T(8,128)S(1)} all-to-all(f32[2,32,32,128]{3,2,0,1:T(8,128)S(1)} %copy.123), channel_id=1, replica_groups=mesh['bank'=4,'lane'=32] {'bank'}, dimensions={1} | all-to-all | bytes 2097152 | tf_op jit(solution)/shard_map/all_to_all | solution.py:57
  143.4 19.5 %all_to_all.145 = f32[2,8,128,128]{2,1,0,3:T(8,128)S(1)} all-to-all(f32[2,8,128,128]{2,1,0,3:T(8,128)S(1)} %copy.126), channel_id=1, replica_groups=mesh['bank'=4,'lane'=32] {'lane'}, dimensions={3} | all-to-all | bytes 2097152 | tf_op jit(solution)/shard_map/all_to_all | solution.py:58
  162.9 1.7 convolution_bitcast_fusion
  165.3 0.7 copy.131
  166.0 19.5 %all_to_all.146 = f32[2,256,128,4]{2,3,0,1:T(4,128)S(1)} all-to-all(f32[2,256,128,4]{2,3,0,1:T(4,128)S(1)} %copy.131), channel_id=1, replica_groups=mesh['bank'=4,'lane'=32] {'lane'}, dimensions={1} | all-to-all | bytes 2097152 | tf_op jit(solution)/shard_map/all_to_all | solution.py:61
  185.7 0.9 copy.134
  186.6 2.1 %add.42 = f32[8,4,32,128]{2,1,0,3:T(4,128)S(1)} reshape(f32[1,8,128,32,4]{2,1,4,3,0:T(8,128)} %copy.134) | data formatting | bytes 1048576 | tf_op jit(solution)/shard_map/add | solution.py:62
  188.6 1.6 copy.135
  190.3 6.5 %all-to-all-start.8 = ((f32[4,8,32,128]{3,2,1,0:T(8,128)}), f32[4,8,32,128]{3,2,1,0:T(8,128)S(1)}, u32[]{:S(2)}, u32[]{:S(2)}) async-start(f32[4,8,32,128]{3,2,1,0:T(8,128)} %copy.135), calls=%async_computation.8 | async-start | bytes 1048576 | tf_op jit(solution)/shard_map/all_to_all | solution.py:17
  197.0 1.4 copy.137
  198.3 7.9 %all-to-all-done.8 = f32[4,8,32,128]{3,2,1,0:T(8,128)S(1)} async-done(((f32[4,8,32,128]{3,2,1,0:T(8,128)}), f32[4,8,32,128]{3,2,1,0:T(8,128)S(1)}, u32[]{:S(2)}, u32[]{:S(2)}) %all-to-all-start.8) | async-done | bytes 524320 | tf_op jit(solution)/shard_map/all_to_all | solution.py:17
  206.5 0.9 copy.138
  (27 shorter events, 5.0 us)
Async XLA Ops:
  8.0 20.8 %all-to-all-start = ((f32[2,8,128,128]{3,1,0,2:T(8,128)}), f32[2,8,128,128]{3,1,0,2:T(8,128)S(1)}, u32[]{:S(2)}, u32[]{:S(2)}) async-start(f32[2,8,128,128]{3,1,0,2:T(8,128)} %copy.98), calls=%async_computation | async-start | bytes 2097152 | tf_op jit(solution)/shard_map/all_to_all | solution.py:55
  96.6 1.0 copy-start
  190.3 15.9 %all-to-all-start.8 = ((f32[4,8,32,128]{3,2,1,0:T(8,128)}), f32[4,8,32,128]{3,2,1,0:T(8,128)S(1)}, u32[]{:S(2)}, u32[]{:S(2)}) async-start(f32[4,8,32,128]{3,2,1,0:T(8,128)} %copy.135), calls=%async_computation.8 | async-start | bytes 1048576 | tf_op jit(solution)/shard_map/all_to_all | solution.py:17
where the time goes:
time: 208 us; the launch traced here: 207 us
  blocking collectives  140 us (67%)
  waiting for transfers between devices  22.8 us (11%)
  local copies, waits for them, and re-layouts  16.3 us (8%)
  starting transfers between devices  12.3 us (6%)
  matrix products  9.65 us (5%)
  other arithmetic  5.36 us (3%)
    all_to_all x2, blocking collectives, shards(): lax.all_to_all(values, 'lane', split_axis=3, concat_axis=1, tiled=True)  44 us
    all_to_all x2, blocking collectives, shards(): lax.all_to_all(moved, 'lane', split_axis=1, concat_axis=3, tiled=True)  38.9 us
    all_to_all x2, blocking collectives, shards(): lax.all_to_all(moved, 'bank', split_axis=1, concat_axis=2, tiled=True)  36.6 us
    all_to_all x1, blocking collectives, shards(): lax.all_to_all(values, 'bank', split_axis=2, concat_axis=1, tiled=True)  20.6 us
    all_to_all x1, waiting for transfers between devices, shards(): lax.all_to_all(values, 'bank', split_axis=2, concat_axis=1, tiled=True)  14.9 us
    dot_general x8, matrix products, apply_along(): jnp.tensordot(values, real_part, axes=([dim], [0]), precision=lax.Precisi...  9.65 us
    all_to_all x1, waiting for transfers between devices, sent_and_summed(): parts = lax.all_to_all(cut_along(shard, dim, size), axis, 0, 0, tiled=True)  7.87 us
    all_to_all x1, starting transfers between devices, sent_and_summed(): parts = lax.all_to_all(cut_along(shard, dim, size), axis, 0, 0, tiled=True)  6.53 us
  transfers between devices with their start and end apart: 2, of which 2 were waited for; matrix products, arithmetic and copies ran while one was open for 1% of the time, Pallas kernels for 0%

commit v1 on v0

v1 whole, which is shorter than its diff:
```python
import functools

import jax
import jax.numpy as jnp
import numpy as np
from jax import lax
from jax.experimental import pallas as pl
from jax.experimental.pallas import tpu as pltpu
from jax.sharding import PartitionSpec as P

F32 = jnp.float32
BF16 = jnp.bfloat16
HALF = 2.0**-12


def fit(parity, terms, reach=2.6):
    k = np.arange(400)
    x = reach * np.cos(np.pi * (k + 0.5) / 400)
    powers = np.stack([x ** (2 * n + parity) for n in range(terms)], 1)
    want = np.sin(x) if parity else np.cos(x)
    scale = np.abs(powers).max(0)
    coef = np.linalg.lstsq(powers / scale, want, rcond=None)[0] / scale
    return [float(c) for c in coef]


SIN, COS = fit(1, 7), fit(0, 8)


def horner(coefs, x2):
    total = jnp.full_like(x2, coefs[-1])
    for c in coefs[-2::-1]:
        total = total * x2 + c
    return total


def turned(re, im, turn):
    x2 = turn * turn
    sin, cos = turn * horner(SIN, x2), horner(COS, x2)
    return re * cos + im * sin, im * cos - re * sin


def walsh(parts):
    parts, step = list(parts), 1
    while step < len(parts):
        for i in range(len(parts)):
            if not i & step:
                u, v = parts[i], parts[i + step]
                parts[i], parts[i + step] = u + v, u - v
        step *= 2
    return parts


def signs():
    both = lax.broadcasted_iota(jnp.int32, (128, 128), 0) & lax.broadcasted_iota(jnp.int32, (128, 128), 1)
    for shift in (4, 2, 1):
        both = both ^ (both >> shift)
    return (1 - 2 * (both & 1)).astype(F32).astype(BF16)


def split(x):
    first = x.astype(BF16)
    rest = x - first.astype(F32)
    second = rest.astype(BF16)
    third = (rest - second.astype(F32)).astype(BF16)
    return [first, second, third]


def mixed(re, im, sign):
    both = jnp.concatenate([re, im], 0)
    right = jnp.concatenate([sign] * 3, 0)
    both = jnp.dot(jnp.concatenate(split(both), 1), right, preferred_element_type=F32)
    both = jnp.concatenate([both[:128], both[128:]], 1)
    left = jnp.concatenate([sign] * 3, 1)
    both = jnp.dot(left, jnp.concatenate(split(both), 0), preferred_element_type=F32)
    return both[:, :128], both[:, 128:]


def first_kernel(amp, ener, angle, out):
    sign = signs()
    a = angle[0:1, :]
    for b in range(8):
        e = ener[b]
        re, im = turned(amp[0, b], amp[1, b], a * e)
        re, im = mixed(re, im, sign)
        out[b * 16 : b * 16 + 16, 0] = re.reshape(16, 8, 128)
        out[b * 16 : b * 16 + 16, 1] = im.reshape(16, 8, 128)
        out[b * 16 : b * 16 + 16, 2] = e.reshape(16, 8, 128)
    for r in range(16):
        for c in range(2):
            for b, part in enumerate(walsh([out[b * 16 + r, c] for b in range(8)])):
                out[b * 16 + r, c] = part


def second_kernel(got, angle, out):
    sign = signs()
    a = angle[1:2, :]
    for r in range(16):
        for c in range(2):
            for b, part in enumerate(walsh([got[b * 16 + r, c] for b in range(8)])):
                out[b * 16 + r, c] = part
    for b in range(8):
        rows = range(b * 16, b * 16 + 16)
        re = jnp.concatenate(walsh([out[r, 0] for r in rows]), 0)
        im = jnp.concatenate(walsh([out[r, 1] for r in rows]), 0)
        e = got[b * 16 : b * 16 + 16, 2].reshape(128, 128)
        re, im = turned(re * HALF, im * HALF, a * e)
        re, im = mixed(re, im, sign)
        out[b * 16 : b * 16 + 16, 0] = re.reshape(16, 8, 128)
        out[b * 16 : b * 16 + 16, 1] = im.reshape(16, 8, 128)
    for r in range(16):
        for c in range(2):
            for b, part in enumerate(walsh([out[b * 16 + r, c] for b in range(8)])):
                out[b * 16 + r, c] = part


def third_kernel(core, got, out, keep, send, held):
    for b in range(8):
        for c in range(2):
            rows = range(b * 16, b * 16 + 16)
            for r, part in zip(rows, walsh([got[r, c] * HALF for r in rows])):
                held[r, c] = part
    mine = core[0] == 0
    for hi in range(2):
        for low in range(4):
            chance = [[], []]
            for co in range(2):
                r = hi * 8 + co * 4 + low
                re = walsh([held[b * 16 + r, 0] for b in range(8)])
                im = walsh([held[b * 16 + r, 1] for b in range(8)])
                for b in range(8):
                    out[0, b, r * 8 : r * 8 + 8, :] = re[b]
                    out[1, b, r * 8 : r * 8 + 8, :] = im[b]
                    chance[co].append((re[b] * re[b] + im[b] * im[b]) * 0.25)
            for b in range(8):
                u, v = chance[0][b], chance[1][b]
                keep[hi, b, low * 8 : low * 8 + 8, :] = jnp.where(mine, u, v)
                send[hi, b, low * 8 : low * 8 + 8, :] = jnp.where(mine, v, u)


def shape(*dims):
    return jax.ShapeDtypeStruct(dims, F32)


VMEM = pl.BlockSpec(memory_space=pltpu.VMEM)
SMEM = pl.BlockSpec(memory_space=pltpu.SMEM)
BOTH = ("bank", "lane")


def shards(amplitudes, energies, diagonal_angles):
    bank = lax.axis_index("bank")
    values = pl.pallas_call(
        first_kernel, out_shape=shape(128, 3, 8, 128), in_specs=[VMEM] * 3, out_specs=VMEM, name="first"
    )(amplitudes, energies, diagonal_angles)
    values = lax.all_to_all(values.reshape(128, 24, 128), BOTH, 0, 0, tiled=True)
    values = pl.pallas_call(
        second_kernel, out_shape=shape(128, 2, 8, 128), in_specs=[VMEM] * 2, out_specs=VMEM, name="second"
    )(values.reshape(128, 3, 8, 128), diagonal_angles)
    values = lax.all_to_all(values.reshape(128, 16, 128), BOTH, 0, 0, tiled=True)
    final, keep, send = pl.pallas_call(
        third_kernel,
        out_shape=(shape(2, 8, 128, 128), shape(2, 8, 32, 128), shape(2, 8, 32, 128)),
        in_specs=[SMEM, VMEM],
        out_specs=(VMEM, VMEM, VMEM),
        scratch_shapes=[pltpu.VMEM((128, 2, 8, 128), F32)],
        name="third",
    )((bank % 2).reshape(1), values.reshape(128, 2, 8, 128))
    got = lax.ppermute(send, "bank", [(i, i ^ 1) for i in range(4)])
    far = bank // 2
    pick = lambda x, i: lax.dynamic_index_in_dim(x, i, 0, keepdims=False)
    away = pick(keep, 1 - far) + pick(got, 1 - far)
    here = pick(keep, far) + pick(got, far)
    marginal = here + lax.ppermute(away, "bank", [(i, i ^ 2) for i in range(4)])
    return final, marginal


def solution(mesh):
    return jax.shard_map(
        shards,
        mesh=mesh,
        in_specs=(P(None, BOTH, None, None), P(BOTH, None, None), P()),
        out_specs=(P(None, BOTH, None, None), P("lane", "bank", None)),
        check_vma=False,
    )
```

time: 208 us -> 86 us (0.41)
  blocking collectives: 140 us -> 36.5 us
  local copies, waits for them, and re-layouts: 16.3 us -> 0.97 us
  Pallas kernels: 0 us -> 12.6 us
  matrix products: 9.65 us -> 0 us
  starting transfers between devices: 12.3 us -> 6.04 us
  waiting for transfers between devices: 22.8 us -> 26.4 us
  other arithmetic: 5.36 us -> 2.51 us
    all_to_all x7 -> x1, blocking collectives: 140 us -> 36.5 us  [shards(): lax.all_to_all(values.reshape(128, 24, 128), BOTH, 0, 0, tiled=True)]
    pallas_call x0 -> x3, Pallas kernels: none -> 12.6 us  [the longest x1 4.95 us: shards(): pl.pallas_call(second_kernel, out_shape=shape(128, 2, 8, 128), in_specs=[...]
    dot_general x8 -> x0, matrix products: 9.65 us -> none  [apply_along(): jnp.tensordot(values, real_part, axes=([dim], [0]), precision=lax.Precisi...]
    all_to_all x2 -> x1, starting transfers between devices: 12.3 us -> 4.39 us  [shards(): lax.all_to_all(values.reshape(128, 16, 128), BOTH, 0, 0, tiled=True)]
    ppermute x0 -> x2, waiting for transfers between devices: none -> 6.93 us  [the longest x1 5.56 us: shards(): marginal = here + lax.ppermute(away, 'bank', [(i, i ^ 2) for i in range(4)])]
    transpose x7 -> x0, local copies, waits for them, and re-layouts: 5.97 us -> none  [the longest x6 4.32 us: apply_along(): return jnp.moveaxis(moved, -1, dim)]
    another operation x2 -> x0, other arithmetic: 5.09 us -> none  [diagonal_step(): jnp.stack([values[0] * jnp.cos(turn) + values[1] * jnp.sin(turn), values[...]
    all_to_all x2 -> x1, waiting for transfers between devices: 22.8 us -> 19.5 us  [shards(): lax.all_to_all(values.reshape(128, 16, 128), BOTH, 0, 0, tiled=True)]
  transfers between devices with their start and end apart: 2 -> 3, of which waited for: 2 -> 3; matrix products, arithmetic and copies ran while one was open for 1% -> 0% of each run, Pallas kernels for 0% -> 0%
where the time goes in v1:
time: 86 us; the launch traced here: 85.6 us
  blocking collectives  36.5 us (42%)
  waiting for transfers between devices  26.4 us (31%)
  Pallas kernels  12.6 us (15%)
  starting transfers between devices  6.04 us (7%)
  other arithmetic  2.51 us (3%)
  local copies, waits for them, and re-layouts  0.97 us (1%)
    all_to_all x1, blocking collectives, shards(): lax.all_to_all(values.reshape(128, 24, 128), BOTH, 0, 0, tiled=True)  36.5 us
    all_to_all x1, waiting for transfers between devices, shards(): lax.all_to_all(values.reshape(128, 16, 128), BOTH, 0, 0, tiled=True)  19.5 us
    ppermute x1, waiting for transfers between devices, shards(): marginal = here + lax.ppermute(away, 'bank', [(i, i ^ 2) for i in range(4)])  5.56 us
    pallas_call x1, Pallas kernels, shards(): pl.pallas_call(second_kernel, out_shape=shape(128, 2, 8, 128), in_specs=[...  4.95 us
    pallas_call x1, Pallas kernels, shards(): pl.pallas_call(first_kernel, out_shape=shape(128, 3, 8, 128), in_specs=[V...  4.78 us
    all_to_all x1, starting transfers between devices, shards(): lax.all_to_all(values.reshape(128, 16, 128), BOTH, 0, 0, tiled=True)  4.39 us
    pallas_call x1, Pallas kernels, shards(): pl.pallas_call(third_kernel, out_shape=(shape(2, 8, 128, 128), shape(2, 8...  2.85 us
  transfers between devices with their start and end apart: 3, of which 3 were waited for; matrix products, arithmetic and copies ran while one was open for 0% of the time, Pallas kernels for 0%

profile of v1, /device:TPU:1, one launch (start us, length us, event | category | flops | bytes accessed | tf_op | source)
XLA Modules:
  0.0 85.6 jit_solution(13587930390001484533)
XLA Ops:
  0.6 4.8 %first.1 = f32[128,3,8,128]{3,2,1,0:T(8,128)} custom-call(f32[2,8,128,128]{3,2,1,0:T(8,128)} %amp.1, f32[8,128,128]{2,1,0:T(8,128)} %ener.1, f32[2,128]{1,0:T(2,128)} %angle.3), custom_call_target="tpu_custom_call" | custom-call | tf_op jit(solution)/shard_map/first/pallas_call | solution.py:151
  5.4 36.5 %all_to_all.10 = f32[128,24,128]{2,1,0:T(8,128)} all-to-all(f32[128,24,128]{2,1,0:T(8,128)} %bitcast.10), channel_id=1, replica_groups=mesh['bank'=4,'lane'=32] {'bank','lane'}, dimensions={0} | all-to-all | bytes 3145728 | tf_op jit(solution)/shard_map/all_to_all | solution.py:154
  41.9 4.9 %second.1 = f32[128,2,8,128]{3,2,1,0:T(8,128)} custom-call(f32[128,3,8,128]{3,2,1,0:T(8,128)} %bitcast.9, f32[2,128]{1,0:T(2,128)} %angle.3), custom_call_target="tpu_custom_call" | custom-call | tf_op jit(solution)/shard_map/second/pallas_call | solution.py:155
  46.8 4.4 %all-to-all-start.1 = ((f32[128,16,128]{2,1,0:T(8,128)}), f32[128,16,128]{2,1,0:T(8,128)S(1)}, u32[]{:S(2)}, u32[]{:S(2)}) async-start(f32[128,16,128]{2,1,0:T(8,128)} %bitcast.11), calls=%async_computation.1 | async-start | bytes 2097152 | tf_op jit(solution)/shard_map/all_to_all | solution.py:158
  51.2 19.5 %all-to-all-done.1 = f32[128,16,128]{2,1,0:T(8,128)S(1)} async-done(((f32[128,16,128]{2,1,0:T(8,128)}), f32[128,16,128]{2,1,0:T(8,128)S(1)}, u32[]{:S(2)}, u32[]{:S(2)}) %all-to-all-start.1) | async-done | bytes 1048608 | tf_op jit(solution)/shard_map/all_to_all | solution.py:158
  70.7 0.0 copy-start
  70.7 1.0 %copy-done = f32[128,16,128]{2,1,0:T(8,128)} copy-done((f32[128,16,128]{2,1,0:T(8,128)}, f32[128,16,128]{2,1,0:T(8,128)S(1)}, u32[]{:S(2)}) %copy-start) | copy-done | bytes 1048600
  71.7 2.9 %third.1 = (f32[2,8,128,128]{3,2,1,0:T(8,128)}, f32[2,8,32,128]{3,2,1,0:T(8,128)}, f32[2,8,32,128]{3,2,1,0:T(8,128)}) custom-call(s32[1]{0:T(128)} %bitcast.core, f32[128,2,8,128]{3,2,1,0:T(8,128)} %bitcast.12), custom_call_target="tpu_custom_call" | custom-call | tf_op jit(solution)/shard_map/third/pallas_call | solution.py:159
  74.5 0.9 %collective-permute-start = (f32[2,8,32,128]{3,2,1,0:T(8,128)}, f32[2,8,32,128]{3,2,1,0:T(8,128)S(1)}, u32[]{:S(2)}, u32[]{:S(2)}) collective-permute-start(f32[2,8,32,128]{3,2,1,0:T(8,128)} %get-tuple-element.7), channel_id=1, source_target_pairs={{0,32},{32,0},{64,96},{96,64},{1,33},{33,1},{65,97},{97,65},{2,34}... | collective-permute-start | bytes 786440 | tf_op jit(solution)/shard_map/ppermute | solution.py:167
  75.5 1.4 %collective-permute-done = f32[2,8,32,128]{3,2,1,0:T(8,128)S(1)} collective-permute-done((f32[2,8,32,128]{3,2,1,0:T(8,128)}, f32[2,8,32,128]{3,2,1,0:T(8,128)S(1)}, u32[]{:S(2)}, u32[]{:S(2)}) %collective-permute-start) | collective-permute-done | bytes 262176 | tf_op jit(solution)/shard_map/ppermute | solution.py:167
  76.8 0.9 %add_bitcast_fusion = f32[8,32,128]{2,1,0:T(8,128)S(1)} fusion(f32[2,8,32,128]{3,2,1,0:T(8,128)S(1)} %collective-permute-done, s32[]{:T(128)S(6)} %select_n.23, f32[2,8,32,128]{3,2,1,0:T(8,128)} %get-tuple-element.6), kind=kLoop, calls=%fused_computation.1 | loop fusion | flops 32768 | bytes 393220 | tf_op jit(solution)/shard_map/add | solution.py:170
  77.8 0.7 collective-permute-start.1
  78.5 5.6 %collective-permute-done.1 = f32[8,32,128]{2,1,0:T(8,128)S(1)} collective-permute-done((f32[8,32,128]{2,1,0:T(8,128)S(1)}, f32[8,32,128]{2,1,0:T(8,128)S(1)}, u32[]{:S(2)}, u32[]{:S(2)}) %collective-permute-start.1) | collective-permute-done | bytes 131104 | tf_op jit(solution)/shard_map/ppermute | solution.py:172
  84.0 1.6 %bitcast_add_fusion = f32[8,32,128]{2,1,0:T(8,128)} fusion(f32[8,32,128]{2,1,0:T(8,128)S(1)} %collective-permute-done.1, f32[2,8,32,128]{3,2,1,0:T(8,128)S(1)} %collective-permute-done, s32[]{:T(128)S(6)} %select_n.22, f32[2,8,32,128]{3,2,1,0:T(8,128)} %get-tuple-element.6), kind=kLoop, calls=%fused_computation | loop fusion | flops 65536 | bytes 524292 | tf_op jit(solution)/shard_map/add | solution.py:172
Async XLA Ops:
  46.8 23.9 %all-to-all-start.1 = ((f32[128,16,128]{2,1,0:T(8,128)}), f32[128,16,128]{2,1,0:T(8,128)S(1)}, u32[]{:S(2)}, u32[]{:S(2)}) async-start(f32[128,16,128]{2,1,0:T(8,128)} %bitcast.11), calls=%async_computation.1 | async-start | bytes 2097152 | tf_op jit(solution)/shard_map/all_to_all | solution.py:158
  70.7 1.0 %copy-start = (f32[128,16,128]{2,1,0:T(8,128)}, f32[128,16,128]{2,1,0:T(8,128)S(1)}, u32[]{:S(2)}) copy-start(f32[128,16,128]{2,1,0:T(8,128)S(1)} %all-to-all-done.1) | copy-start | bytes 3145732
  74.5 2.3 %collective-permute-start = (f32[2,8,32,128]{3,2,1,0:T(8,128)}, f32[2,8,32,128]{3,2,1,0:T(8,128)S(1)}, u32[]{:S(2)}, u32[]{:S(2)}) collective-permute-start(f32[2,8,32,128]{3,2,1,0:T(8,128)} %get-tuple-element.7), channel_id=1, source_target_pairs={{0,32},{32,0},{64,96},{96,64},{1,33},{33,1},{65,97},{97,65},{2,34}... | collective-permute-start | bytes 786440 | tf_op jit(solution)/shard_map/ppermute | solution.py:167
  77.8 6.3 %collective-permute-start.1 = (f32[8,32,128]{2,1,0:T(8,128)S(1)}, f32[8,32,128]{2,1,0:T(8,128)S(1)}, u32[]{:S(2)}, u32[]{:S(2)}) collective-permute-start(f32[8,32,128]{2,1,0:T(8,128)S(1)} %add_bitcast_fusion), channel_id=1, source_target_pairs={{0,64},{32,96},{64,0},{96,32},{1,65},{33,97},{65,1},{97,33},{2,66}... | collective-permute-start | bytes 393224 | tf_op jit(solution)/shard_map/ppermute | solution.py:172

commit v2 on v1

--- a/solution.py
+++ b/solution.py
@@ -1,5 +1,3 @@
-import functools
-
 import jax
 import jax.numpy as jnp
 import numpy as np
@@ -75,16 +73,28 @@
     return both[:, :128], both[:, 128:]
 
 
-def first_kernel(amp, ener, angle, out):
+def first_kernel(amp, ener, angle, out, arrived):
+    def copies(b):
+        rows = pl.ds(b * 16, 16)
+        return [
+            pltpu.make_async_copy(amp.at[0, b], out.at[rows, 0], arrived.at[b, 0]),
+            pltpu.make_async_copy(amp.at[1, b], out.at[rows, 1], arrived.at[b, 1]),
+            pltpu.make_async_copy(ener.at[b], out.at[rows, 2], arrived.at[b, 2]),
+        ]
+
+    for b in range(8):
+        for copy in copies(b):
+            copy.start()
     sign = signs()
     a = angle[0:1, :]
     for b in range(8):
-        e = ener[b]
-        re, im = turned(amp[0, b], amp[1, b], a * e)
+        for copy in copies(b):
+            copy.wait()
+        re, im, e = (out[b * 16 : b * 16 + 16, c].reshape(128, 128) for c in range(3))
+        re, im = turned(re, im, a * e)
         re, im = mixed(re, im, sign)
         out[b * 16 : b * 16 + 16, 0] = re.reshape(16, 8, 128)
         out[b * 16 : b * 16 + 16, 1] = im.reshape(16, 8, 128)
-        out[b * 16 : b * 16 + 16, 2] = e.reshape(16, 8, 128)
     for r in range(16):
         for c in range(2):
             for b, part in enumerate(walsh([out[b * 16 + r, c] for b in range(8)])):
@@ -113,63 +123,68 @@
                 out[b * 16 + r, c] = part
 
 
-def third_kernel(core, got, out, keep, send, held):
+def third_kernel(place, got, out, keep, send, held):
+    for r in range(16):
+        for c in range(2):
+            for b, part in enumerate(walsh([got[b * 16 + r, c] * HALF for b in range(8)])):
+                held[b * 16 + r, c] = part
+    mine = (place[0] & 1) == 0
+    far = place[0] >> 1
     for b in range(8):
-        for c in range(2):
-            rows = range(b * 16, b * 16 + 16)
-            for r, part in zip(rows, walsh([got[r, c] * HALF for r in rows])):
-                held[r, c] = part
-    mine = core[0] == 0
-    for hi in range(2):
-        for low in range(4):
-            chance = [[], []]
-            for co in range(2):
-                r = hi * 8 + co * 4 + low
-                re = walsh([held[b * 16 + r, 0] for b in range(8)])
-                im = walsh([held[b * 16 + r, 1] for b in range(8)])
-                for b in range(8):
-                    out[0, b, r * 8 : r * 8 + 8, :] = re[b]
-                    out[1, b, r * 8 : r * 8 + 8, :] = im[b]
-                    chance[co].append((re[b] * re[b] + im[b] * im[b]) * 0.25)
-            for b in range(8):
-                u, v = chance[0][b], chance[1][b]
-                keep[hi, b, low * 8 : low * 8 + 8, :] = jnp.where(mine, u, v)
-                send[hi, b, low * 8 : low * 8 + 8, :] = jnp.where(mine, v, u)
+        chance = []
+        re = walsh([held[b * 16 + r, 0] for r in range(16)])
+        im = walsh([held[b * 16 + r, 1] for r in range(16)])
+        for r in range(16):
+            out[0, b, r * 8 : r * 8 + 8, :] = re[r]
+            out[1, b, r * 8 : r * 8 + 8, :] = im[r]
+            chance.append((re[r] * re[r] + im[r] * im[r]) * 0.25)
+        for hi in range(2):
+            for low in range(4):
+                u, v = chance[hi * 8 + low], chance[hi * 8 + 4 + low]
+                keep[hi ^ far, b, low * 8 : low * 8 + 8, :] = jnp.where(mine, u, v)
+                send[hi ^ far, b, low * 8 : low * 8 + 8, :] = jnp.where(mine, v, u)
 
 
-def shape(*dims):
-    return jax.ShapeDtypeStruct(dims, F32)
+def here(*dims):
+    return pltpu.VMEM(dims, F32)
+
+
+def near(x):
+    return pltpu.with_memory_space_constraint(x, pltpu.VMEM)
 
 
 VMEM = pl.BlockSpec(memory_space=pltpu.VMEM)
 SMEM = pl.BlockSpec(memory_space=pltpu.SMEM)
+HBM = pl.BlockSpec(memory_space=pltpu.HBM)
 BOTH = ("bank", "lane")
+ORDER = ("lane", "bank")
 
 
 def shards(amplitudes, energies, diagonal_angles):
-    bank = lax.axis_index("bank")
+    diagonal_angles, bank = lax.optimization_barrier((diagonal_angles, lax.axis_index("bank")))
     values = pl.pallas_call(
-        first_kernel, out_shape=shape(128, 3, 8, 128), in_specs=[VMEM] * 3, out_specs=VMEM, name="first"
-    )(amplitudes, energies, diagonal_angles)
-    values = lax.all_to_all(values.reshape(128, 24, 128), BOTH, 0, 0, tiled=True)
+        first_kernel,
+        out_shape=here(128, 3, 8, 128),
+        in_specs=[HBM, HBM, VMEM],
+        out_specs=VMEM,
+        scratch_shapes=[pltpu.SemaphoreType.DMA((8, 3))],
+        name="first",
+    )(amplitudes.reshape(2, 8, 16, 8, 128), energies.reshape(8, 16, 8, 128), diagonal_angles)
+    values = lax.all_to_all(values.reshape(128, 24, 128), ORDER, 0, 0, tiled=True)
     values = pl.pallas_call(
-        second_kernel, out_shape=shape(128, 2, 8, 128), in_specs=[VMEM] * 2, out_specs=VMEM, name="second"
-    )(values.reshape(128, 3, 8, 128), diagonal_angles)
-    values = lax.all_to_all(values.reshape(128, 16, 128), BOTH, 0, 0, tiled=True)
+        second_kernel, out_shape=here(128, 2, 8, 128), in_specs=[VMEM] * 2, out_specs=VMEM, name="second"
+    )(near(values.reshape(128, 3, 8, 128)), diagonal_angles)
+    values = lax.all_to_all(values.reshape(128, 16, 128), ORDER, 0, 0, tiled=True)
     final, keep, send = pl.pallas_call(
         third_kernel,
-        out_shape=(shape(2, 8, 128, 128), shape(2, 8, 32, 128), shape(2, 8, 32, 128)),
+        out_shape=(here(2, 8, 128, 128), here(2, 8, 32, 128), here(2, 8, 32, 128)),
         in_specs=[SMEM, VMEM],
         out_specs=(VMEM, VMEM, VMEM),
         scratch_shapes=[pltpu.VMEM((128, 2, 8, 128), F32)],
         name="third",
-    )((bank % 2).reshape(1), values.reshape(128, 2, 8, 128))
+    )(bank.reshape(1), near(values.reshape(128, 2, 8, 128)))
     got = lax.ppermute(send, "bank", [(i, i ^ 1) for i in range(4)])
-    far = bank // 2
-    pick = lambda x, i: lax.dynamic_index_in_dim(x, i, 0, keepdims=False)
-    away = pick(keep, 1 - far) + pick(got, 1 - far)
-    here = pick(keep, far) + pick(got, far)
-    marginal = here + lax.ppermute(away, "bank", [(i, i ^ 2) for i in range(4)])
+    marginal = keep[0] + got[0] + lax.ppermute(keep[1] + got[1], "bank", [(i, i ^ 2) for i in range(4)])
     return final, marginal
 
 

time: 86 us -> 77.9 us (0.906)
  blocking collectives: 36.5 us -> 58.8 us
  waiting for transfers between devices: 26.4 us -> 5.18 us
  starting transfers between devices: 6.04 us -> 2.17 us
  Pallas kernels: 12.6 us -> 9.19 us
  other arithmetic: 2.51 us -> 0.71 us
    all_to_all x1 -> x2, blocking collectives: 36.5 us -> 58.8 us  [the longest x1 35.7 us: shards(): lax.all_to_all(values.reshape(128, 24, 128), ORDER, 0, 0, tiled=True)]
    all_to_all x1 -> x0, waiting for transfers between devices: 19.5 us -> none  [shards(): lax.all_to_all(values.reshape(128, 16, 128), BOTH, 0, 0, tiled=True)]
    all_to_all x1 -> x0, starting transfers between devices: 4.39 us -> none  [shards(): lax.all_to_all(values.reshape(128, 16, 128), BOTH, 0, 0, tiled=True)]
    pallas_call x3, Pallas kernels: 12.6 us -> 9.19 us  [the longest x1 5.48 us: shards(): pl.pallas_call(first_kernel, out_shape=here(128, 3, 8, 128), in_specs=[HB...]
    add x2, other arithmetic: 2.51 us -> 0.71 us  [the longest x1 0.69 us: shards(): keep[0] + got[0]]
    ppermute x1, waiting for transfers between devices: 5.56 us -> 4.02 us  [shards(): lax.ppermute(keep[1] + got[1], 'bank', [(i, i ^ 2) for i in range(4)])]
  transfers between devices with their start and end apart: 3 -> 2, of which waited for: 3 -> 2; matrix products, arithmetic and copies ran while one was open for 0% -> 1% of each run, Pallas kernels for 0% -> 0%
where the time goes in v2:
time: 77.9 us; the launch traced here: 77.7 us
  blocking collectives  58.8 us (75%)
  Pallas kernels  9.19 us (12%)
  waiting for transfers between devices  5.18 us (7%)
  starting transfers between devices  2.17 us (3%)
  local copies, waits for them, and re-layouts  0.97 us (1%)
    all_to_all x1, blocking collectives, shards(): lax.all_to_all(values.reshape(128, 24, 128), ORDER, 0, 0, tiled=True)  35.7 us
    all_to_all x1, blocking collectives, shards(): lax.all_to_all(values.reshape(128, 16, 128), ORDER, 0, 0, tiled=True)  23.2 us
    pallas_call x1, Pallas kernels, shards(): pl.pallas_call(first_kernel, out_shape=here(128, 3, 8, 128), in_specs=[HB...  5.48 us
    ppermute x1, waiting for transfers between devices, shards(): lax.ppermute(keep[1] + got[1], 'bank', [(i, i ^ 2) for i in range(4)])  4.02 us
    pallas_call x1, Pallas kernels, shards(): pl.pallas_call(second_kernel, out_shape=here(128, 2, 8, 128), in_specs=[V...  3.24 us
  transfers between devices with their start and end apart: 2, of which 2 were waited for; matrix products, arithmetic and copies ran while one was open for 1% of the time, Pallas kernels for 0%

profile of v2, /device:TPU:1, one launch (start us, length us, event | category | flops | bytes accessed | tf_op | source)
XLA Modules:
  0.0 77.7 jit_solution(4182373617112759977)
XLA Ops:
  0.6 5.5 %first.1 = f32[128,3,8,128]{3,2,1,0:T(8,128)S(1)} custom-call(f32[2,8,16,8,128]{4,3,2,1,0:T(8,128)} %bitcast.17, f32[8,16,8,128]{3,2,1,0:T(8,128)} %bitcast.18, f32[2,128]{1,0:T(2,128)} %angle.1), custom_call_target="tpu_custom_call" | custom-call | tf_op jit(solution)/shard_map/first/pallas_call | solution.py:165
  6.1 35.7 %all_to_all.10 = f32[128,24,128]{2,1,0:T(8,128)S(1)} all-to-all(f32[128,24,128]{2,1,0:T(8,128)S(1)} %bitcast.14), channel_id=1, replica_groups=mesh['bank'=4,'lane'=32] {'lane','bank'}, dimensions={0} | all-to-all | bytes 3145728 | tf_op jit(solution)/shard_map/all_to_all | solution.py:173
  41.8 3.2 %second.1 = f32[128,2,8,128]{3,2,1,0:T(8,128)S(1)} custom-call(f32[128,3,8,128]{3,2,1,0:T(8,128)S(1)} %bitcast.13, f32[2,128]{1,0:T(2,128)} %angle.1), custom_call_target="tpu_custom_call" | custom-call | tf_op jit(solution)/shard_map/second/pallas_call | solution.py:174
  45.0 23.2 %all_to_all.11 = f32[128,16,128]{2,1,0:T(8,128)S(1)} all-to-all(f32[128,16,128]{2,1,0:T(8,128)S(1)} %bitcast.15), channel_id=1, replica_groups=mesh['bank'=4,'lane'=32] {'lane','bank'}, dimensions={0} | all-to-all | bytes 2097152 | tf_op jit(solution)/shard_map/all_to_all | solution.py:177
  68.2 0.5 third.1
  68.7 0.9 %collective-permute-start = (f32[2,8,32,128]{3,2,1,0:T(8,128)S(1)}, f32[2,8,32,128]{3,2,1,0:T(8,128)S(1)}, u32[]{:S(2)}, u32[]{:S(2)}) collective-permute-start(f32[2,8,32,128]{3,2,1,0:T(8,128)S(1)} %get-tuple-element.11), channel_id=1, source_target_pairs={{0,32},{32,0},{64,96},{96,64},{1,33},{33,1},{65,97},{97,65},{2,34}... | collective-permute-start | bytes 786440 | tf_op jit(solution)/shard_map/ppermute | solution.py:186
  69.6 1.2 %collective-permute-done = f32[2,8,32,128]{3,2,1,0:T(8,128)S(1)} collective-permute-done((f32[2,8,32,128]{3,2,1,0:T(8,128)S(1)}, f32[2,8,32,128]{3,2,1,0:T(8,128)S(1)}, u32[]{:S(2)}, u32[]{:S(2)}) %collective-permute-start) | collective-permute-done | bytes 262176 | tf_op jit(solution)/shard_map/ppermute | solution.py:186
  70.8 1.3 %collective-permute-start.1 = (f32[8,32,128]{2,1,0:T(8,128)S(1)}, f32[8,32,128]{2,1,0:T(8,128)S(1)}, u32[]{:S(2)}, u32[]{:S(2)}) collective-permute-start(f32[8,32,128]{2,1,0:T(8,128)S(1)} %fusion), channel_id=1, source_target_pairs={{0,64},{32,96},{64,0},{96,32},{1,65},{33,97},{65,1},{97,33},{2,66}... | collective-permute-start | bytes 393224 | tf_op jit(solution)/shard_map/ppermute | solution.py:187
  72.0 1.0 %copy.5 = f32[2,8,128,128]{3,2,1,0:T(8,128)} copy(f32[2,8,128,128]{3,2,1,0:T(8,128)S(1)} %get-tuple-element.12) | data formatting | bytes 2097152
  73.0 4.0 %collective-permute-done.1 = f32[8,32,128]{2,1,0:T(8,128)S(1)} collective-permute-done((f32[8,32,128]{2,1,0:T(8,128)S(1)}, f32[8,32,128]{2,1,0:T(8,128)S(1)}, u32[]{:S(2)}, u32[]{:S(2)}) %collective-permute-start.1) | collective-permute-done | bytes 131104 | tf_op jit(solution)/shard_map/ppermute | solution.py:187
  77.0 0.7 fusion.2
  (1 shorter events, 0.0 us)
Async XLA Ops:
  68.7 2.1 %collective-permute-start = (f32[2,8,32,128]{3,2,1,0:T(8,128)S(1)}, f32[2,8,32,128]{3,2,1,0:T(8,128)S(1)}, u32[]{:S(2)}, u32[]{:S(2)}) collective-permute-start(f32[2,8,32,128]{3,2,1,0:T(8,128)S(1)} %get-tuple-element.11), channel_id=1, source_target_pairs={{0,32},{32,0},{64,96},{96,64},{1,33},{33,1},{65,97},{97,65},{2,34}... | collective-permute-start | bytes 786440 | tf_op jit(solution)/shard_map/ppermute | solution.py:186
  70.8 6.3 %collective-permute-start.1 = (f32[8,32,128]{2,1,0:T(8,128)S(1)}, f32[8,32,128]{2,1,0:T(8,128)S(1)}, u32[]{:S(2)}, u32[]{:S(2)}) collective-permute-start(f32[8,32,128]{2,1,0:T(8,128)S(1)} %fusion), channel_id=1, source_target_pairs={{0,64},{32,96},{64,0},{96,32},{1,65},{33,97},{65,1},{97,33},{2,66}... | collective-permute-start | bytes 393224 | tf_op jit(solution)/shard_map/ppermute | solution.py:187

commit v3 on v2

v3 whole, which is shorter than its diff:
```python
import jax
import jax.numpy as jnp
import numpy as np
from jax import lax
from jax.experimental import pallas as pl
from jax.experimental.pallas import tpu as pltpu
from jax.sharding import PartitionSpec as P

F32 = jnp.float32
BF16 = jnp.bfloat16
GROUP = 4
HALF = 2.0**-12


def fit(parity, terms, reach=2.6):
    k = np.arange(400)
    x = reach * np.cos(np.pi * (k + 0.5) / 400)
    powers = np.stack([x ** (2 * n + parity) for n in range(terms)], 1)
    want = np.sin(x) if parity else np.cos(x)
    scale = np.abs(powers).max(0)
    coef = np.linalg.lstsq(powers / scale, want, rcond=None)[0] / scale
    return [float(c) for c in coef]


SIN, COS = fit(1, 7), fit(0, 8)


def horner(coefs, x2):
    total = jnp.full_like(x2, coefs[-1])
    for c in coefs[-2::-1]:
        total = total * x2 + c
    return total


def turned(re, im, turn):
    x2 = turn * turn
    sin, cos = turn * horner(SIN, x2), horner(COS, x2)
    return re * cos + im * sin, im * cos - re * sin


def walsh(parts):
    parts, step = list(parts), 1
    while step < len(parts):
        for i in range(len(parts)):
            if not i & step:
                u, v = parts[i], parts[i + step]
                parts[i], parts[i + step] = u + v, u - v
        step *= 2
    return parts


def signs():
    both = lax.broadcasted_iota(jnp.int32, (128, 128), 0) & lax.broadcasted_iota(jnp.int32, (128, 128), 1)
    for shift in (4, 2, 1):
        both = both ^ (both >> shift)
    return (1 - 2 * (both & 1)).astype(F32).astype(BF16)


PIECES = 3


def mixed(re, im, sign):
    rest = jnp.concatenate([re, im], 0)
    pieces = []
    for _ in range(PIECES):
        pieces.append(rest.astype(BF16))
        rest = rest - pieces[-1].astype(F32)
    both = jnp.dot(jnp.concatenate(pieces, 1), jnp.concatenate([sign] * PIECES, 0), preferred_element_type=F32)
    return both[:128], both[128:]


def tiles(x):
    return [x[r * 8 : r * 8 + 8] for r in range(x.shape[0] // 8)]


def first_kernel(amp, ener, angle, out, held, state, arrived):
    def copies(b):
        return [
            pltpu.make_async_copy(amp.at[0, b], held.at[b, 0], arrived.at[b, 0]),
            pltpu.make_async_copy(amp.at[1, b], held.at[b, 1], arrived.at[b, 1]),
            pltpu.make_async_copy(ener.at[b], held.at[b, 2], arrived.at[b, 2]),
        ]

    for b in range(8):
        for copy in copies(b):
            copy.start()
    sign = signs()
    a = angle[0:1, :]
    for b in range(8):
        if b % GROUP == 0:
            for near_by in range(b, b + GROUP):
                for copy in copies(near_by):
                    copy.wait()
        re, im = turned(held[b, 0], held[b, 1], a * held[b, 2])
        for c, part in enumerate(mixed(re, im, sign)):
            for r, tile in enumerate(walsh(tiles(part))):
                state[b * 2 + c, r * 8 : r * 8 + 8, :] = tile
        for top in range(2):
            for low in range(8):
                out[b * 16 + top * 8 + low, 2] = held[b, 2, pl.ds(top * 64 + low, 8, stride=8), :]
            for c in range(2):
                rows = [state[b * 2 + c, pl.ds(top * 64 + low, 8, stride=8), :] for low in range(8)]
                for low, tile in enumerate(walsh(rows)):
                    out[b * 16 + top * 8 + low, c] = tile
    for r in range(16):
        for c in range(2):
            for b, tile in enumerate(walsh([out[b * 16 + r, c] for b in range(8)])):
                out[b * 16 + r, c] = tile


def second_kernel(got, angle, out):
    sign = signs()
    a = angle[1:2, :]
    for r in range(16):
        for c in range(2):
            for b, tile in enumerate(walsh([got[b * 16 + r, c] * HALF for b in range(8)])):
                out[b * 16 + r, c] = tile
    for b in range(8):
        rows = range(b * 16, b * 16 + 16)
        re = jnp.concatenate(walsh([out[r, 0] for r in rows]), 0)
        im = jnp.concatenate(walsh([out[r, 1] for r in rows]), 0)
        e = got[b * 16 : b * 16 + 16, 2].reshape(128, 128)
        re, im = turned(re, im, a * e)
        for c, part in enumerate(mixed(re, im, sign)):
            for r, tile in zip(rows, walsh(tiles(part))):
                out[r, c] = tile
    for r in range(16):
        for c in range(2):
            for b, tile in enumerate(walsh([out[b * 16 + r, c] for b in range(8)])):
                out[b * 16 + r, c] = tile


def third_kernel(place, got, out, keep, send, held, state):
    for r in range(16):
        for c in range(2):
            for b, tile in enumerate(walsh([got[b * 16 + r, c] * HALF for b in range(8)])):
                held[b * 16 + r, c] = tile
    mine = (place[0] & 1) == 0
    far = place[0] >> 1
    for b in range(8):
        final = []
        for c in range(2):
            for r, tile in enumerate(walsh([held[b * 16 + r, c] for r in range(16)])):
                state[b * 2 + c, pl.ds(r // 8 * 64 + r % 8, 8, stride=8), :] = tile
            both = []
            for top in range(2):
                both += walsh([state[b * 2 + c, top * 64 + mid * 8 : top * 64 + mid * 8 + 8, :] for mid in range(8)])
            for r, tile in enumerate(both):
                out[c, b, r * 8 : r * 8 + 8, :] = tile
            final.append(both)
        chance = [(re * re + im * im) * 0.25 for re, im in zip(*final)]
        for hi in range(2):
            for low in range(4):
                u, v = chance[hi * 8 + low], chance[hi * 8 + 4 + low]
                keep[hi ^ far, b, low * 8 : low * 8 + 8, :] = jnp.where(mine, u, v)
                send[hi ^ far, b, low * 8 : low * 8 + 8, :] = jnp.where(mine, v, u)


def here(*dims):
    return pltpu.VMEM(dims, F32)


def near(x):
    return pltpu.with_memory_space_constraint(x, pltpu.VMEM)


VMEM = pl.BlockSpec(memory_space=pltpu.VMEM)
SMEM = pl.BlockSpec(memory_space=pltpu.SMEM)
HBM = pl.BlockSpec(memory_space=pltpu.HBM)
BOTH = ("bank", "lane")
ORDER = ("lane", "bank")


def shards(amplitudes, energies, diagonal_angles):
    diagonal_angles, bank = lax.optimization_barrier((diagonal_angles, lax.axis_index("bank")))
    values = pl.pallas_call(
        first_kernel,
        out_shape=here(128, 3, 8, 128),
        in_specs=[HBM, HBM, VMEM],
        out_specs=VMEM,
        scratch_shapes=[here(8, 3, 128, 128), here(16, 128, 128), pltpu.SemaphoreType.DMA((8, 3))],
        name="first",
    )(amplitudes, energies, diagonal_angles)
    values = lax.all_to_all(values.reshape(128, 24, 128), ORDER, 0, 0, tiled=True)
    values = pl.pallas_call(
        second_kernel, out_shape=here(128, 2, 8, 128), in_specs=[VMEM] * 2, out_specs=VMEM, name="second"
    )(near(values.reshape(128, 3, 8, 128)), diagonal_angles)
    values = lax.all_to_all(values.reshape(128, 16, 128), ORDER, 0, 0, tiled=True)
    final, keep, send = pl.pallas_call(
        third_kernel,
        out_shape=(here(2, 8, 128, 128), here(2, 8, 32, 128), here(2, 8, 32, 128)),
        in_specs=[SMEM, VMEM],
        out_specs=(VMEM, VMEM, VMEM),
        scratch_shapes=[here(128, 2, 8, 128), here(16, 128, 128)],
        name="third",
    )(bank.reshape(1), near(values.reshape(128, 2, 8, 128)))
    got = lax.ppermute(send, "bank", [(i, i ^ 1) for i in range(4)])
    marginal = keep[0] + got[0] + lax.ppermute(keep[1] + got[1], "bank", [(i, i ^ 2) for i in range(4)])
    return final, marginal


def solution(mesh):
    return jax.shard_map(
        shards,
        mesh=mesh,
        in_specs=(P(None, BOTH, None, None), P(BOTH, None, None), P()),
        out_specs=(P(None, BOTH, None, None), P("lane", "bank", None)),
        check_vma=False,
    )
```

time: 77.9 us -> 75.3 us (0.967)
  Pallas kernels: 9.19 us -> 6.55 us
    pallas_call x1, Pallas kernels: 5.48 us -> 3.61 us  [shards(): pl.pallas_call(first_kernel, out_shape=here(128, 3, 8, 128), in_specs=[HB...]
    pallas_call x1, Pallas kernels: 3.24 us -> 2.36 us  [shards(): pl.pallas_call(second_kernel, out_shape=here(128, 2, 8, 128), in_specs=[V...]
where the time goes in v3:
time: 75.3 us; the launch traced here: 75.1 us
  blocking collectives  58.8 us (78%)
  Pallas kernels  6.55 us (9%)
  waiting for transfers between devices  5.18 us (7%)
  starting transfers between devices  2.17 us (3%)
  local copies, waits for them, and re-layouts  0.97 us (1%)
    all_to_all x1, blocking collectives, shards(): lax.all_to_all(values.reshape(128, 24, 128), ORDER, 0, 0, tiled=True)  35.7 us
    all_to_all x1, blocking collectives, shards(): lax.all_to_all(values.reshape(128, 16, 128), ORDER, 0, 0, tiled=True)  23.2 us
    ppermute x1, waiting for transfers between devices, shards(): lax.ppermute(keep[1] + got[1], 'bank', [(i, i ^ 2) for i in range(4)])  4.02 us
    pallas_call x1, Pallas kernels, shards(): pl.pallas_call(first_kernel, out_shape=here(128, 3, 8, 128), in_specs=[HB...  3.61 us
    pallas_call x1, Pallas kernels, shards(): pl.pallas_call(second_kernel, out_shape=here(128, 2, 8, 128), in_specs=[V...  2.36 us
  transfers between devices with their start and end apart: 2, of which 2 were waited for; matrix products, arithmetic and copies ran while one was open for 1% of the time, Pallas kernels for 0%

profile of v3, /device:TPU:1, one launch (start us, length us, event | category | flops | bytes accessed | tf_op | source)
XLA Modules:
  0.0 75.1 jit_solution(7500603758560927188)
XLA Ops:
  0.6 3.6 %first.1 = f32[128,3,8,128]{3,2,1,0:T(8,128)S(1)} custom-call(f32[2,8,128,128]{3,2,1,0:T(8,128)} %amp.1, f32[8,128,128]{2,1,0:T(8,128)} %ener.1, f32[2,128]{1,0:T(2,128)} %angle.1), custom_call_target="tpu_custom_call" | custom-call | tf_op jit(solution)/shard_map/first/pallas_call | solution.py:176
  4.3 35.7 %all_to_all.10 = f32[128,24,128]{2,1,0:T(8,128)S(1)} all-to-all(f32[128,24,128]{2,1,0:T(8,128)S(1)} %bitcast.12), channel_id=1, replica_groups=mesh['bank'=4,'lane'=32] {'lane','bank'}, dimensions={0} | all-to-all | bytes 3145728 | tf_op jit(solution)/shard_map/all_to_all | solution.py:184
  39.9 2.4 %second.1 = f32[128,2,8,128]{3,2,1,0:T(8,128)S(1)} custom-call(f32[128,3,8,128]{3,2,1,0:T(8,128)S(1)} %bitcast.11, f32[2,128]{1,0:T(2,128)} %angle.1), custom_call_target="tpu_custom_call" | custom-call | tf_op jit(solution)/shard_map/second/pallas_call | solution.py:185
  42.3 23.2 %all_to_all.11 = f32[128,16,128]{2,1,0:T(8,128)S(1)} all-to-all(f32[128,16,128]{2,1,0:T(8,128)S(1)} %bitcast.13), channel_id=1, replica_groups=mesh['bank'=4,'lane'=32] {'lane','bank'}, dimensions={0} | all-to-all | bytes 2097152 | tf_op jit(solution)/shard_map/all_to_all | solution.py:188
  65.5 0.6 third.1
  66.0 0.9 %collective-permute-start = (f32[2,8,32,128]{3,2,1,0:T(8,128)S(1)}, f32[2,8,32,128]{3,2,1,0:T(8,128)S(1)}, u32[]{:S(2)}, u32[]{:S(2)}) collective-permute-start(f32[2,8,32,128]{3,2,1,0:T(8,128)S(1)} %get-tuple-element.11), channel_id=1, source_target_pairs={{0,32},{32,0},{64,96},{96,64},{1,33},{33,1},{65,97},{97,65},{2,34}... | collective-permute-start | bytes 786440 | tf_op jit(solution)/shard_map/ppermute | solution.py:197
  66.9 1.2 %collective-permute-done = f32[2,8,32,128]{3,2,1,0:T(8,128)S(1)} collective-permute-done((f32[2,8,32,128]{3,2,1,0:T(8,128)S(1)}, f32[2,8,32,128]{3,2,1,0:T(8,128)S(1)}, u32[]{:S(2)}, u32[]{:S(2)}) %collective-permute-start) | collective-permute-done | bytes 262176 | tf_op jit(solution)/shard_map/ppermute | solution.py:197
  68.1 1.3 %collective-permute-start.1 = (f32[8,32,128]{2,1,0:T(8,128)S(1)}, f32[8,32,128]{2,1,0:T(8,128)S(1)}, u32[]{:S(2)}, u32[]{:S(2)}) collective-permute-start(f32[8,32,128]{2,1,0:T(8,128)S(1)} %fusion), channel_id=1, source_target_pairs={{0,64},{32,96},{64,0},{96,32},{1,65},{33,97},{65,1},{97,33},{2,66}... | collective-permute-start | bytes 393224 | tf_op jit(solution)/shard_map/ppermute | solution.py:198
  69.4 1.0 %copy.5 = f32[2,8,128,128]{3,2,1,0:T(8,128)} copy(f32[2,8,128,128]{3,2,1,0:T(8,128)S(1)} %get-tuple-element.12) | data formatting | bytes 2097152
  70.4 4.0 %collective-permute-done.1 = f32[8,32,128]{2,1,0:T(8,128)S(1)} collective-permute-done((f32[8,32,128]{2,1,0:T(8,128)S(1)}, f32[8,32,128]{2,1,0:T(8,128)S(1)}, u32[]{:S(2)}, u32[]{:S(2)}) %collective-permute-start.1) | collective-permute-done | bytes 131104 | tf_op jit(solution)/shard_map/ppermute | solution.py:198
  74.4 0.7 fusion.2
  (1 shorter events, 0.0 us)
Async XLA Ops:
  66.0 2.1 %collective-permute-start = (f32[2,8,32,128]{3,2,1,0:T(8,128)S(1)}, f32[2,8,32,128]{3,2,1,0:T(8,128)S(1)}, u32[]{:S(2)}, u32[]{:S(2)}) collective-permute-start(f32[2,8,32,128]{3,2,1,0:T(8,128)S(1)} %get-tuple-element.11), channel_id=1, source_target_pairs={{0,32},{32,0},{64,96},{96,64},{1,33},{33,1},{65,97},{97,65},{2,34}... | collective-permute-start | bytes 786440 | tf_op jit(solution)/shard_map/ppermute | solution.py:197
  68.1 6.3 %collective-permute-start.1 = (f32[8,32,128]{2,1,0:T(8,128)S(1)}, f32[8,32,128]{2,1,0:T(8,128)S(1)}, u32[]{:S(2)}, u32[]{:S(2)}) collective-permute-start(f32[8,32,128]{2,1,0:T(8,128)S(1)} %fusion), channel_id=1, source_target_pairs={{0,64},{32,96},{64,0},{96,32},{1,65},{33,97},{65,1},{97,33},{2,66}... | collective-permute-start | bytes 393224 | tf_op jit(solution)/shard_map/ppermute | solution.py:198

commit v4 on v3

--- a/solution.py
+++ b/solution.py
@@ -5,6 +5,7 @@
 from jax.experimental import pallas as pl
 from jax.experimental.pallas import tpu as pltpu
 from jax.sharding import PartitionSpec as P
+
 
 F32 = jnp.float32
 BF16 = jnp.bfloat16
@@ -111,6 +112,7 @@
 def second_kernel(got, angle, out):
     sign = signs()
     a = angle[1:2, :]
+    upper = lax.broadcasted_iota(jnp.int32, (8, 128), 0) < 4
     for r in range(16):
         for c in range(2):
             for b, tile in enumerate(walsh([got[b * 16 + r, c] * HALF for b in range(8)])):
@@ -122,38 +124,56 @@
         e = got[b * 16 : b * 16 + 16, 2].reshape(128, 128)
         re, im = turned(re, im, a * e)
         for c, part in enumerate(mixed(re, im, sign)):
-            for r, tile in zip(rows, walsh(tiles(part))):
-                out[r, c] = tile
+            mid = walsh(tiles(part))
+            for r in range(0, 16, 2):
+                u = jnp.where(upper, mid[r], pltpu.roll(mid[r + 1], 4, 0))
+                v = jnp.where(upper, pltpu.roll(mid[r], 4, 0), mid[r + 1])
+                out[b * 16 + r, c] = u + v
+                out[b * 16 + r + 1, c] = u - v
     for r in range(16):
         for c in range(2):
             for b, tile in enumerate(walsh([out[b * 16 + r, c] for b in range(8)])):
                 out[b * 16 + r, c] = tile
 
 
-def third_kernel(place, got, out, keep, send, held, state):
+def third_kernel(place, got, mine, away, keep, send, held, state):
     for r in range(16):
         for c in range(2):
             for b, tile in enumerate(walsh([got[b * 16 + r, c] * HALF for b in range(8)])):
                 held[b * 16 + r, c] = tile
-    mine = (place[0] & 1) == 0
-    far = place[0] >> 1
-    for b in range(8):
-        final = []
+    core = (place[0] & 1) == 0
+    far = (place[0] >> 1) == 0
+    for b in range(8):
+        chance = []
         for c in range(2):
             for r, tile in enumerate(walsh([held[b * 16 + r, c] for r in range(16)])):
                 state[b * 2 + c, pl.ds(r // 8 * 64 + r % 8, 8, stride=8), :] = tile
-            both = []
             for top in range(2):
-                both += walsh([state[b * 2 + c, top * 64 + mid * 8 : top * 64 + mid * 8 + 8, :] for mid in range(8)])
-            for r, tile in enumerate(both):
-                out[c, b, r * 8 : r * 8 + 8, :] = tile
-            final.append(both)
-        chance = [(re * re + im * im) * 0.25 for re, im in zip(*final)]
-        for hi in range(2):
-            for low in range(4):
-                u, v = chance[hi * 8 + low], chance[hi * 8 + 4 + low]
-                keep[hi ^ far, b, low * 8 : low * 8 + 8, :] = jnp.where(mine, u, v)
-                send[hi ^ far, b, low * 8 : low * 8 + 8, :] = jnp.where(mine, v, u)
+                both = []
+                for half in range(2):
+                    rows = [top * 64 + half * 32 + mid * 8 for mid in range(4)]
+                    both.append(walsh([state[b * 2 + c, r : r + 8, :] for r in rows]))
+                for mid, (u, v) in enumerate(zip(*both)):
+                    mine[c, b, top, mid * 8 : mid * 8 + 8, :] = jnp.where(core, u, v)
+                    away[c, b, top, mid * 8 : mid * 8 + 8, :] = jnp.where(core, v, u)
+                    chance.append(u * u + v * v)
+        for mid in range(4):
+            u = (chance[mid] + chance[8 + mid]) * 0.25
+            v = (chance[4 + mid] + chance[12 + mid]) * 0.25
+            keep[b, mid * 8 : mid * 8 + 8, :] = jnp.where(far, u, v)
+            send[b, mid * 8 : mid * 8 + 8, :] = jnp.where(far, v, u)
+
+
+def last_kernel(place, mine, other, out, done):
+    core = place[0] & 1
+    copies = []
+    for c in range(2):
+        copies.append(pltpu.make_async_copy(mine.at[c], out.at[c, :, :, core], done.at[0, c]))
+        copies.append(pltpu.make_async_copy(other.at[c], out.at[c, :, :, 1 - core], done.at[1, c]))
+    for copy in copies:
+        copy.start()
+    for copy in copies:
+        copy.wait()
 
 
 def here(*dims):
@@ -186,17 +206,27 @@
         second_kernel, out_shape=here(128, 2, 8, 128), in_specs=[VMEM] * 2, out_specs=VMEM, name="second"
     )(near(values.reshape(128, 3, 8, 128)), diagonal_angles)
     values = lax.all_to_all(values.reshape(128, 16, 128), ORDER, 0, 0, tiled=True)
-    final, keep, send = pl.pallas_call(
+    place = bank.reshape(1)
+    mine, away, keep, send = pl.pallas_call(
         third_kernel,
-        out_shape=(here(2, 8, 128, 128), here(2, 8, 32, 128), here(2, 8, 32, 128)),
+        out_shape=(here(2, 8, 2, 32, 128), here(2, 8, 2, 32, 128), here(8, 32, 128), here(8, 32, 128)),
         in_specs=[SMEM, VMEM],
-        out_specs=(VMEM, VMEM, VMEM),
+        out_specs=(VMEM,) * 4,
         scratch_shapes=[here(128, 2, 8, 128), here(16, 128, 128)],
         name="third",
-    )(bank.reshape(1), near(values.reshape(128, 2, 8, 128)))
-    got = lax.ppermute(send, "bank", [(i, i ^ 1) for i in range(4)])
-    marginal = keep[0] + got[0] + lax.ppermute(keep[1] + got[1], "bank", [(i, i ^ 2) for i in range(4)])
-    return final, marginal
+    )(place, near(values.reshape(128, 2, 8, 128)))
+    other = lax.ppermute(away, "bank", [(i, i ^ 1) for i in range(4)])
+    final = pl.pallas_call(
+        last_kernel,
+        out_shape=jax.ShapeDtypeStruct((2, 8, 2, 2, 32, 128), F32),
+        in_specs=[SMEM, VMEM, VMEM],
+        out_specs=HBM,
+        scratch_shapes=[pltpu.SemaphoreType.DMA((2, 2))],
+        name="last",
+    )(place, near(mine), near(other))
+    sent = lax.ppermute(send, "bank", [(i, i ^ 2) for i in range(4)])
+    marginal = keep + sent
+    return final.reshape(2, 8, 128, 128), marginal
 
 
 def solution(mesh):

time: 75.3 us -> 75.4 us (level)
  Pallas kernels: 6.55 us -> 7.66 us
  local copies, waits for them, and re-layouts: 0.97 us -> 0 us
    pallas_call x1 -> x2, Pallas kernels: 0.58 us -> 1.58 us  [the longest x1 0.99 us: shards(): pl.pallas_call(last_kernel, out_shape=jax.ShapeDtypeStruct((2, 8, 2, 2, 3...]
    unnamed x1 -> x0, local copies, waits for them, and re-layouts: 0.97 us -> none
  transfers between devices with their start and end apart: 2 -> 2, of which waited for: 2 -> 1; matrix products, arithmetic and copies ran while one was open for 1% -> 1% of each run, Pallas kernels for 0% -> 0%
where the time goes in v4:
time: 75.4 us; the launch traced here: 75.2 us
  blocking collectives  58.8 us (78%)
  Pallas kernels  7.66 us (10%)
  waiting for transfers between devices  5.28 us (7%)
  starting transfers between devices  2.09 us (3%)
    all_to_all x1, blocking collectives, shards(): lax.all_to_all(values.reshape(128, 24, 128), ORDER, 0, 0, tiled=True)  35.7 us
    all_to_all x1, blocking collectives, shards(): lax.all_to_all(values.reshape(128, 16, 128), ORDER, 0, 0, tiled=True)  23.2 us
    ppermute x1, waiting for transfers between devices, shards(): sent = lax.ppermute(send, 'bank', [(i, i ^ 2) for i in range(4)])  5.27 us
    pallas_call x1, Pallas kernels, shards(): pl.pallas_call(first_kernel, out_shape=here(128, 3, 8, 128), in_specs=[HB...  3.61 us
    pallas_call x1, Pallas kernels, shards(): pl.pallas_call(second_kernel, out_shape=here(128, 2, 8, 128), in_specs=[V...  2.47 us
  transfers between devices with their start and end apart: 2, of which 1 were waited for; matrix products, arithmetic and copies ran while one was open for 1% of the time, Pallas kernels for 0%

profile of v4, /device:TPU:1, one launch (start us, length us, event | category | flops | bytes accessed | tf_op | source)
XLA Modules:
  0.0 75.2 jit_solution(16418120497812202424)
XLA Ops:
  0.6 3.6 %first.1 = f32[128,3,8,128]{3,2,1,0:T(8,128)S(1)} custom-call(f32[2,8,128,128]{3,2,1,0:T(8,128)} %amp.1, f32[8,128,128]{2,1,0:T(8,128)} %ener.1, f32[2,128]{1,0:T(2,128)} %angle.1), custom_call_target="tpu_custom_call" | custom-call | tf_op jit(solution)/shard_map/first/pallas_call | solution.py:196
  4.3 35.7 %all_to_all.10 = f32[128,24,128]{2,1,0:T(8,128)S(1)} all-to-all(f32[128,24,128]{2,1,0:T(8,128)S(1)} %bitcast.7), channel_id=1, replica_groups=mesh['bank'=4,'lane'=32] {'lane','bank'}, dimensions={0} | all-to-all | bytes 3145728 | tf_op jit(solution)/shard_map/all_to_all | solution.py:204
  39.9 2.5 %second.1 = f32[128,2,8,128]{3,2,1,0:T(8,128)S(1)} custom-call(f32[128,3,8,128]{3,2,1,0:T(8,128)S(1)} %bitcast.6, f32[2,128]{1,0:T(2,128)} %angle.1), custom_call_target="tpu_custom_call" | custom-call | tf_op jit(solution)/shard_map/second/pallas_call | solution.py:205
  42.4 23.2 %all_to_all.11 = f32[128,16,128]{2,1,0:T(8,128)S(1)} all-to-all(f32[128,16,128]{2,1,0:T(8,128)S(1)} %bitcast.8), channel_id=1, replica_groups=mesh['bank'=4,'lane'=32] {'lane','bank'}, dimensions={0} | all-to-all | bytes 2097152 | tf_op jit(solution)/shard_map/all_to_all | solution.py:208
  65.6 0.6 third.1
  66.2 0.9 %collective-permute-start = (f32[2,8,2,32,128]{4,3,2,1,0:T(8,128)S(1)}, f32[2,8,2,32,128]{4,3,2,1,0:T(8,128)S(1)}, u32[]{:S(2)}, u32[]{:S(2)}) collective-permute-start(f32[2,8,2,32,128]{4,3,2,1,0:T(8,128)S(1)} %get-tuple-element.11), channel_id=1, source_target_pairs={{0,32},{32,0},{64,96},{96,64},{1,33},{33,1},{65,97},{97,65},{2,34}... | collective-permute-start | bytes 1572872 | tf_op jit(solution)/shard_map/ppermute | solution.py:218
  67.1 1.2 %collective-permute-start.1 = (f32[8,32,128]{2,1,0:T(8,128)S(1)}, f32[8,32,128]{2,1,0:T(8,128)S(1)}, u32[]{:S(2)}, u32[]{:S(2)}) collective-permute-start(f32[8,32,128]{2,1,0:T(8,128)S(1)} %get-tuple-element.13), channel_id=1, source_target_pairs={{0,64},{32,96},{64,0},{96,32},{1,65},{33,97},{65,1},{97,33},{2,66}... | collective-permute-start | bytes 393224 | tf_op jit(solution)/shard_map/ppermute | solution.py:227
  68.3 5.3 %collective-permute-done.1 = f32[8,32,128]{2,1,0:T(8,128)S(1)} collective-permute-done((f32[8,32,128]{2,1,0:T(8,128)S(1)}, f32[8,32,128]{2,1,0:T(8,128)S(1)}, u32[]{:S(2)}, u32[]{:S(2)}) %collective-permute-start.1) | collective-permute-done | bytes 131104 | tf_op jit(solution)/shard_map/ppermute | solution.py:227
  73.5 0.7 add.3
  74.2 0.0 collective-permute-done.other
  74.2 1.0 %last.1 = f32[2,8,2,2,32,128]{5,4,3,2,1,0:T(8,128)} custom-call(s32[1]{0:T(128)} %bitcast.place, f32[2,8,2,32,128]{4,3,2,1,0:T(8,128)S(1)} %get-tuple-element.10.mine, f32[2,8,2,32,128]{4,3,2,1,0:T(8,128)S(1)} %collective-permute-done.other), custom_call_target="tpu_custom_call" | custom-call | tf_op jit(solution)/shard_map/last/pallas_call | solution.py:219
Async XLA Ops:
  66.2 8.0 %collective-permute-start = (f32[2,8,2,32,128]{4,3,2,1,0:T(8,128)S(1)}, f32[2,8,2,32,128]{4,3,2,1,0:T(8,128)S(1)}, u32[]{:S(2)}, u32[]{:S(2)}) collective-permute-start(f32[2,8,2,32,128]{4,3,2,1,0:T(8,128)S(1)} %get-tuple-element.11), channel_id=1, source_target_pairs={{0,32},{32,0},{64,96},{96,64},{1,33},{33,1},{65,97},{97,65},{2,34}... | collective-permute-start | bytes 1572872 | tf_op jit(solution)/shard_map/ppermute | solution.py:218
  67.1 6.5 %collective-permute-start.1 = (f32[8,32,128]{2,1,0:T(8,128)S(1)}, f32[8,32,128]{2,1,0:T(8,128)S(1)}, u32[]{:S(2)}, u32[]{:S(2)}) collective-permute-start(f32[8,32,128]{2,1,0:T(8,128)S(1)} %get-tuple-element.13), channel_id=1, source_target_pairs={{0,64},{32,96},{64,0},{96,32},{1,65},{33,97},{65,1},{97,33},{2,66}... | collective-permute-start | bytes 393224 | tf_op jit(solution)/shard_map/ppermute | solution.py:227

commit v5 on v4

--- a/solution.py
+++ b/solution.py
@@ -9,33 +9,30 @@
 
 F32 = jnp.float32
 BF16 = jnp.bfloat16
-GROUP = 4
-HALF = 2.0**-12
-
-
-def fit(parity, terms, reach=2.6):
+GROUPS = (2, 3, 3)
+SCALE = 2.0**-13
+
+
+def fit(terms, reach):
     k = np.arange(400)
     x = reach * np.cos(np.pi * (k + 0.5) / 400)
-    powers = np.stack([x ** (2 * n + parity) for n in range(terms)], 1)
-    want = np.sin(x) if parity else np.cos(x)
+    powers = np.stack([x ** (2 * n + 1) for n in range(terms)], 1)
     scale = np.abs(powers).max(0)
-    coef = np.linalg.lstsq(powers / scale, want, rcond=None)[0] / scale
-    return [float(c) for c in coef]
-
-
-SIN, COS = fit(1, 7), fit(0, 8)
-
-
-def horner(coefs, x2):
-    total = jnp.full_like(x2, coefs[-1])
-    for c in coefs[-2::-1]:
-        total = total * x2 + c
-    return total
-
-
-def turned(re, im, turn):
-    x2 = turn * turn
-    sin, cos = turn * horner(SIN, x2), horner(COS, x2)
+    return [float(c) for c in np.linalg.lstsq(powers / scale, 2 * np.sin(x), rcond=None)[0] / scale]
+
+
+SIN = fit(6, 1.4)
+
+
+def turned(re, im, half):
+    square = half * half
+    sin = jnp.full_like(half, SIN[-1])
+    for c in SIN[-2::-1]:
+        sin = sin * square + c
+    sin = sin * half
+    square = sin * sin
+    rest = 4.0 - square
+    cos, sin = 2.0 - square, sin * (rest * lax.rsqrt(rest))
     return re * cos + im * sin, im * cos - re * sin
 
 
@@ -54,10 +51,10 @@
     both = lax.broadcasted_iota(jnp.int32, (128, 128), 0) & lax.broadcasted_iota(jnp.int32, (128, 128), 1)
     for shift in (4, 2, 1):
         both = both ^ (both >> shift)
-    return (1 - 2 * (both & 1)).astype(F32).astype(BF16)
-
-
-PIECES = 3
+    return ((1 - 2 * (both & 1)).astype(F32) * SCALE).astype(BF16)
+
+
+PIECES = 2
 
 
 def mixed(re, im, sign):
@@ -85,12 +82,13 @@
     for b in range(8):
         for copy in copies(b):
             copy.start()
+    starts = {sum(GROUPS[:i]): size for i, size in enumerate(GROUPS)}
     sign = signs()
-    a = angle[0:1, :]
-    for b in range(8):
-        if b % GROUP == 0:
-            for near_by in range(b, b + GROUP):
-                for copy in copies(near_by):
+    a = angle[0:1, :] * 0.5
+    for b in range(8):
+        if b in starts:
+            for ready in range(b, b + starts[b]):
+                for copy in copies(ready):
                     copy.wait()
         re, im = turned(held[b, 0], held[b, 1], a * held[b, 2])
         for c, part in enumerate(mixed(re, im, sign)):
@@ -111,11 +109,11 @@
 
 def second_kernel(got, angle, out):
     sign = signs()
-    a = angle[1:2, :]
+    a = angle[1:2, :] * 0.5
     upper = lax.broadcasted_iota(jnp.int32, (8, 128), 0) < 4
     for r in range(16):
         for c in range(2):
-            for b, tile in enumerate(walsh([got[b * 16 + r, c] * HALF for b in range(8)])):
+            for b, tile in enumerate(walsh([got[b * 16 + r, c] for b in range(8)])):
                 out[b * 16 + r, c] = tile
     for b in range(8):
         rows = range(b * 16, b * 16 + 16)
@@ -139,7 +137,7 @@
 def third_kernel(place, got, mine, away, keep, send, held, state):
     for r in range(16):
         for c in range(2):
-            for b, tile in enumerate(walsh([got[b * 16 + r, c] * HALF for b in range(8)])):
+            for b, tile in enumerate(walsh([got[b * 16 + r, c] for b in range(8)])):
                 held[b * 16 + r, c] = tile
     core = (place[0] & 1) == 0
     far = (place[0] >> 1) == 0

time: 75.4 us -> 74.7 us (level)
  no operation moved by 1% of the time
where the time goes in v5:
time: 74.7 us; the launch traced here: 74.5 us
  blocking collectives  58.8 us (79%)
  Pallas kernels  6.93 us (9%)
  waiting for transfers between devices  5.28 us (7%)
  starting transfers between devices  2.09 us (3%)
    all_to_all x1, blocking collectives, shards(): lax.all_to_all(values.reshape(128, 24, 128), ORDER, 0, 0, tiled=True)  35.7 us
    all_to_all x1, blocking collectives, shards(): lax.all_to_all(values.reshape(128, 16, 128), ORDER, 0, 0, tiled=True)  23.2 us
    ppermute x1, waiting for transfers between devices, shards(): sent = lax.ppermute(send, 'bank', [(i, i ^ 2) for i in range(4)])  5.27 us
    pallas_call x1, Pallas kernels, shards(): pl.pallas_call(first_kernel, out_shape=here(128, 3, 8, 128), in_specs=[HB...  3.26 us
    pallas_call x1, Pallas kernels, shards(): pl.pallas_call(second_kernel, out_shape=here(128, 2, 8, 128), in_specs=[V...  2.11 us
  transfers between devices with their start and end apart: 2, of which 1 were waited for; matrix products, arithmetic and copies ran while one was open for 1% of the time, Pallas kernels for 0%

profile of v5, /device:TPU:1, one launch (start us, length us, event | category | flops | bytes accessed | tf_op | source)
XLA Modules:
  0.0 74.5 jit_solution(17489590264863317730)
XLA Ops:
  0.6 3.3 %first.1 = f32[128,3,8,128]{3,2,1,0:T(8,128)S(1)} custom-call(f32[2,8,128,128]{3,2,1,0:T(8,128)} %amp.1, f32[8,128,128]{2,1,0:T(8,128)} %ener.1, f32[2,128]{1,0:T(2,128)} %angle.1), custom_call_target="tpu_custom_call" | custom-call | tf_op jit(solution)/shard_map/first/pallas_call | solution.py:194
  3.9 35.7 %all_to_all.10 = f32[128,24,128]{2,1,0:T(8,128)S(1)} all-to-all(f32[128,24,128]{2,1,0:T(8,128)S(1)} %bitcast.7), channel_id=1, replica_groups=mesh['bank'=4,'lane'=32] {'lane','bank'}, dimensions={0} | all-to-all | bytes 3145728 | tf_op jit(solution)/shard_map/all_to_all | solution.py:202
  39.6 2.1 %second.1 = f32[128,2,8,128]{3,2,1,0:T(8,128)S(1)} custom-call(f32[128,3,8,128]{3,2,1,0:T(8,128)S(1)} %bitcast.6, f32[2,128]{1,0:T(2,128)} %angle.1), custom_call_target="tpu_custom_call" | custom-call | tf_op jit(solution)/shard_map/second/pallas_call | solution.py:203
  41.7 23.2 %all_to_all.11 = f32[128,16,128]{2,1,0:T(8,128)S(1)} all-to-all(f32[128,16,128]{2,1,0:T(8,128)S(1)} %bitcast.8), channel_id=1, replica_groups=mesh['bank'=4,'lane'=32] {'lane','bank'}, dimensions={0} | all-to-all | bytes 2097152 | tf_op jit(solution)/shard_map/all_to_all | solution.py:206
  64.9 0.6 third.1
  65.4 0.9 %collective-permute-start = (f32[2,8,2,32,128]{4,3,2,1,0:T(8,128)S(1)}, f32[2,8,2,32,128]{4,3,2,1,0:T(8,128)S(1)}, u32[]{:S(2)}, u32[]{:S(2)}) collective-permute-start(f32[2,8,2,32,128]{4,3,2,1,0:T(8,128)S(1)} %get-tuple-element.11), channel_id=1, source_target_pairs={{0,32},{32,0},{64,96},{96,64},{1,33},{33,1},{65,97},{97,65},{2,34}... | collective-permute-start | bytes 1572872 | tf_op jit(solution)/shard_map/ppermute | solution.py:216
  66.3 1.2 %collective-permute-start.1 = (f32[8,32,128]{2,1,0:T(8,128)S(1)}, f32[8,32,128]{2,1,0:T(8,128)S(1)}, u32[]{:S(2)}, u32[]{:S(2)}) collective-permute-start(f32[8,32,128]{2,1,0:T(8,128)S(1)} %get-tuple-element.13), channel_id=1, source_target_pairs={{0,64},{32,96},{64,0},{96,32},{1,65},{33,97},{65,1},{97,33},{2,66}... | collective-permute-start | bytes 393224 | tf_op jit(solution)/shard_map/ppermute | solution.py:225
  67.5 5.3 %collective-permute-done.1 = f32[8,32,128]{2,1,0:T(8,128)S(1)} collective-permute-done((f32[8,32,128]{2,1,0:T(8,128)S(1)}, f32[8,32,128]{2,1,0:T(8,128)S(1)}, u32[]{:S(2)}, u32[]{:S(2)}) %collective-permute-start.1) | collective-permute-done | bytes 131104 | tf_op jit(solution)/shard_map/ppermute | solution.py:225
  72.8 0.7 add.3
  73.5 0.0 collective-permute-done.other
  73.5 1.0 %last.1 = f32[2,8,2,2,32,128]{5,4,3,2,1,0:T(8,128)} custom-call(s32[1]{0:T(128)} %bitcast.place, f32[2,8,2,32,128]{4,3,2,1,0:T(8,128)S(1)} %get-tuple-element.10.mine, f32[2,8,2,32,128]{4,3,2,1,0:T(8,128)S(1)} %collective-permute-done.other), custom_call_target="tpu_custom_call" | custom-call | tf_op jit(solution)/shard_map/last/pallas_call | solution.py:217
Async XLA Ops:
  65.4 8.0 %collective-permute-start = (f32[2,8,2,32,128]{4,3,2,1,0:T(8,128)S(1)}, f32[2,8,2,32,128]{4,3,2,1,0:T(8,128)S(1)}, u32[]{:S(2)}, u32[]{:S(2)}) collective-permute-start(f32[2,8,2,32,128]{4,3,2,1,0:T(8,128)S(1)} %get-tuple-element.11), channel_id=1, source_target_pairs={{0,32},{32,0},{64,96},{96,64},{1,33},{33,1},{65,97},{97,65},{2,34}... | collective-permute-start | bytes 1572872 | tf_op jit(solution)/shard_map/ppermute | solution.py:216
  66.3 6.5 %collective-permute-start.1 = (f32[8,32,128]{2,1,0:T(8,128)S(1)}, f32[8,32,128]{2,1,0:T(8,128)S(1)}, u32[]{:S(2)}, u32[]{:S(2)}) collective-permute-start(f32[8,32,128]{2,1,0:T(8,128)S(1)} %get-tuple-element.13), channel_id=1, source_target_pairs={{0,64},{32,96},{64,0},{96,32},{1,65},{33,97},{65,1},{97,33},{2,66}... | collective-permute-start | bytes 393224 | tf_op jit(solution)/shard_map/ppermute | solution.py:225

commit v6 on v5

--- a/solution.py
+++ b/solution.py
@@ -4,7 +4,7 @@
 from jax import lax
 from jax.experimental import pallas as pl
 from jax.experimental.pallas import tpu as pltpu
-from jax.sharding import PartitionSpec as P
+from jax.sharding import Mesh, PartitionSpec as P
 
 
 F32 = jnp.float32
@@ -107,31 +107,28 @@
                 out[b * 16 + r, c] = tile
 
 
-def second_kernel(got, angle, out):
+def second_kernel(got, angle, out, held, state):
     sign = signs()
     a = angle[1:2, :] * 0.5
-    upper = lax.broadcasted_iota(jnp.int32, (8, 128), 0) < 4
     for r in range(16):
-        for c in range(2):
-            for b, tile in enumerate(walsh([got[b * 16 + r, c] for b in range(8)])):
-                out[b * 16 + r, c] = tile
-    for b in range(8):
-        rows = range(b * 16, b * 16 + 16)
-        re = jnp.concatenate(walsh([out[r, 0] for r in rows]), 0)
-        im = jnp.concatenate(walsh([out[r, 1] for r in rows]), 0)
-        e = got[b * 16 : b * 16 + 16, 2].reshape(128, 128)
+        rows = [r // 8 * 64 + high * 8 + r % 8 for high in range(8)]
+        for c in range(2):
+            for row, tile in zip(rows, walsh([got[row, c] for row in rows])):
+                held[row, c] = tile
+    for high in range(8):
+        rows = [core * 64 + high * 8 + low for core in range(2) for low in range(8)]
+        re = jnp.concatenate(walsh([held[row, 0] for row in rows]), 0)
+        im = jnp.concatenate(walsh([held[row, 1] for row in rows]), 0)
+        e = jnp.concatenate([got[row, 2] for row in rows], 0)
         re, im = turned(re, im, a * e)
         for c, part in enumerate(mixed(re, im, sign)):
-            mid = walsh(tiles(part))
-            for r in range(0, 16, 2):
-                u = jnp.where(upper, mid[r], pltpu.roll(mid[r + 1], 4, 0))
-                v = jnp.where(upper, pltpu.roll(mid[r], 4, 0), mid[r + 1])
-                out[b * 16 + r, c] = u + v
-                out[b * 16 + r + 1, c] = u - v
-    for r in range(16):
-        for c in range(2):
-            for b, tile in enumerate(walsh([out[b * 16 + r, c] for b in range(8)])):
-                out[b * 16 + r, c] = tile
+            for r, tile in enumerate(walsh(tiles(part))):
+                state[c, high * 8 + r % 8, pl.ds(r // 8, 8, stride=2), :] = tile
+    for low in range(8):
+        for c in range(2):
+            parts = [state[c, high * 8 + low, r5 * 8 : r5 * 8 + 8, :] for r5 in range(2) for high in range(8)]
+            for r, tile in enumerate(walsh(parts)):
+                out[r // 8 * 64 + r % 8 * 8 + low, c] = tile
 
 
 def third_kernel(place, got, mine, away, keep, send, held, state):
@@ -149,7 +146,7 @@
             for top in range(2):
                 both = []
                 for half in range(2):
-                    rows = [top * 64 + half * 32 + mid * 8 for mid in range(4)]
+                    rows = [top * 64 + mid * 16 + half * 8 for mid in range(4)]
                     both.append(walsh([state[b * 2 + c, r : r + 8, :] for r in rows]))
                 for mid, (u, v) in enumerate(zip(*both)):
                     mine[c, b, top, mid * 8 : mid * 8 + 8, :] = jnp.where(core, u, v)
@@ -185,12 +182,13 @@
 VMEM = pl.BlockSpec(memory_space=pltpu.VMEM)
 SMEM = pl.BlockSpec(memory_space=pltpu.SMEM)
 HBM = pl.BlockSpec(memory_space=pltpu.HBM)
-BOTH = ("bank", "lane")
-ORDER = ("lane", "bank")
+BANK = ("x_hi", "core")
+LANE = ("z", "y", "x_lo")
+ORDER = ("core", "y", "x_hi", "x_lo", "z")
 
 
 def shards(amplitudes, energies, diagonal_angles):
-    diagonal_angles, bank = lax.optimization_barrier((diagonal_angles, lax.axis_index("bank")))
+    diagonal_angles, bank = lax.optimization_barrier((diagonal_angles, lax.axis_index(BANK)))
     values = pl.pallas_call(
         first_kernel,
         out_shape=here(128, 3, 8, 128),
@@ -201,7 +199,12 @@
     )(amplitudes, energies, diagonal_angles)
     values = lax.all_to_all(values.reshape(128, 24, 128), ORDER, 0, 0, tiled=True)
     values = pl.pallas_call(
-        second_kernel, out_shape=here(128, 2, 8, 128), in_specs=[VMEM] * 2, out_specs=VMEM, name="second"
+        second_kernel,
+        out_shape=here(128, 2, 8, 128),
+        in_specs=[VMEM] * 2,
+        out_specs=VMEM,
+        scratch_shapes=[here(128, 2, 8, 128), here(2, 64, 16, 128)],
+        name="second",
     )(near(values.reshape(128, 3, 8, 128)), diagonal_angles)
     values = lax.all_to_all(values.reshape(128, 16, 128), ORDER, 0, 0, tiled=True)
     place = bank.reshape(1)
@@ -213,7 +216,7 @@
         scratch_shapes=[here(128, 2, 8, 128), here(16, 128, 128)],
         name="third",
     )(place, near(values.reshape(128, 2, 8, 128)))
-    other = lax.ppermute(away, "bank", [(i, i ^ 1) for i in range(4)])
+    other = lax.ppermute(away, "core", [(0, 1), (1, 0)])
     final = pl.pallas_call(
         last_kernel,
         out_shape=jax.ShapeDtypeStruct((2, 8, 2, 2, 32, 128), F32),
@@ -222,16 +225,17 @@
         scratch_shapes=[pltpu.SemaphoreType.DMA((2, 2))],
         name="last",
     )(place, near(mine), near(other))
-    sent = lax.ppermute(send, "bank", [(i, i ^ 2) for i in range(4)])
+    sent = lax.ppermute(send, "x_hi", [(0, 1), (1, 0)])
     marginal = keep + sent
     return final.reshape(2, 8, 128, 128), marginal
 
 
 def solution(mesh):
+    mesh = Mesh(mesh.devices.reshape(2, 2, 4, 4, 2), BANK + LANE)
     return jax.shard_map(
         shards,
         mesh=mesh,
-        in_specs=(P(None, BOTH, None, None), P(BOTH, None, None), P()),
-        out_specs=(P(None, BOTH, None, None), P("lane", "bank", None)),
+        in_specs=(P(None, BANK + LANE, None, None), P(BANK + LANE, None, None), P()),
+        out_specs=(P(None, BANK + LANE, None, None), P(LANE, BANK, None)),
         check_vma=False,
     )

time: 74.7 us -> 74.3 us (level)
  blocking collectives: 58.8 us -> 58 us
    all_to_all x1, blocking collectives: 35.7 us -> 34.2 us  [shards(): lax.all_to_all(values.reshape(128, 24, 128), ORDER, 0, 0, tiled=True)]
where the time goes in v6:
time: 74.3 us; the launch traced here: 74 us
  blocking collectives  58 us (78%)
  Pallas kernels  6.91 us (9%)
  waiting for transfers between devices  5.62 us (8%)
  starting transfers between devices  2.21 us (3%)
    all_to_all x1, blocking collectives, shards(): lax.all_to_all(values.reshape(128, 24, 128), ORDER, 0, 0, tiled=True)  34.2 us
    all_to_all x1, blocking collectives, shards(): lax.all_to_all(values.reshape(128, 16, 128), ORDER, 0, 0, tiled=True)  23.8 us
    ppermute x1, waiting for transfers between devices, shards(): sent = lax.ppermute(send, 'x_hi', [(0, 1), (1, 0)])  5.62 us
    pallas_call x1, Pallas kernels, shards(): pl.pallas_call(first_kernel, out_shape=here(128, 3, 8, 128), in_specs=[HB...  3.26 us
    pallas_call x1, Pallas kernels, shards(): pl.pallas_call(second_kernel, out_shape=here(128, 2, 8, 128), in_specs=[V...  2.09 us
  transfers between devices with their start and end apart: 2, of which 1 were waited for; matrix products, arithmetic and copies ran while one was open for 1% of the time, Pallas kernels for 0%

profile of v6, /device:TPU:1, one launch (start us, length us, event | category | flops | bytes accessed | tf_op | source)
XLA Modules:
  0.0 74.0 jit_solution(8560260416612485377)
XLA Ops:
  0.6 3.3 %first.1 = f32[128,3,8,128]{3,2,1,0:T(8,128)S(1)} custom-call(f32[2,8,128,128]{3,2,1,0:T(8,128)} %amp.1, f32[8,128,128]{2,1,0:T(8,128)} %ener.1, f32[2,128]{1,0:T(2,128)} %angle.1), custom_call_target="tpu_custom_call" | custom-call | tf_op jit(solution)/shard_map/first/pallas_call | solution.py:192
  3.9 34.2 %all_to_all.10 = f32[128,24,128]{2,1,0:T(8,128)S(1)} all-to-all(f32[128,24,128]{2,1,0:T(8,128)S(1)} %bitcast.7), channel_id=1, replica_groups=mesh['x_hi'=2,'core'=2,'z'=4,'y'=4,'x_lo'=2] {'core','y','x_hi','x_lo','z'}, dimensions={0} | all-to-all | bytes 3145728 | tf_op jit(solution)/shard_map/all_to_all | solution.py:200
  38.1 2.1 %second.1 = f32[128,2,8,128]{3,2,1,0:T(8,128)S(1)} custom-call(f32[128,3,8,128]{3,2,1,0:T(8,128)S(1)} %bitcast.6, f32[2,128]{1,0:T(2,128)} %angle.1), custom_call_target="tpu_custom_call" | custom-call | tf_op jit(solution)/shard_map/second/pallas_call | solution.py:201
  40.2 23.8 %all_to_all.11 = f32[128,16,128]{2,1,0:T(8,128)S(1)} all-to-all(f32[128,16,128]{2,1,0:T(8,128)S(1)} %bitcast.8), channel_id=1, replica_groups=mesh['x_hi'=2,'core'=2,'z'=4,'y'=4,'x_lo'=2] {'core','y','x_hi','x_lo','z'}, dimensions={0} | all-to-all | bytes 2097152 | tf_op jit(solution)/shard_map/all_to_all | solution.py:209
  64.0 0.6 third.1
  64.5 1.4 %collective-permute-start = (f32[2,8,2,32,128]{4,3,2,1,0:T(8,128)S(1)}, f32[2,8,2,32,128]{4,3,2,1,0:T(8,128)S(1)}, u32[]{:S(2)}, u32[]{:S(2)}) collective-permute-start(f32[2,8,2,32,128]{4,3,2,1,0:T(8,128)S(1)} %get-tuple-element.11), channel_id=1, source_target_pairs={{0,32},{32,0},{1,33},{33,1},{2,34},{34,2},{3,35},{35,3},{4,36},{36... | collective-permute-start | bytes 1572872 | tf_op jit(solution)/shard_map/ppermute | solution.py:219
  65.9 0.8 %collective-permute-start.1 = (f32[8,32,128]{2,1,0:T(8,128)S(1)}, f32[8,32,128]{2,1,0:T(8,128)S(1)}, u32[]{:S(2)}, u32[]{:S(2)}) collective-permute-start(f32[8,32,128]{2,1,0:T(8,128)S(1)} %get-tuple-element.13), channel_id=1, source_target_pairs={{0,64},{64,0},{1,65},{65,1},{2,66},{66,2},{3,67},{67,3},{4,68},{68... | collective-permute-start | bytes 393224 | tf_op jit(solution)/shard_map/ppermute | solution.py:228
  66.7 5.6 %collective-permute-done.1 = f32[8,32,128]{2,1,0:T(8,128)S(1)} collective-permute-done((f32[8,32,128]{2,1,0:T(8,128)S(1)}, f32[8,32,128]{2,1,0:T(8,128)S(1)}, u32[]{:S(2)}, u32[]{:S(2)}) %collective-permute-start.1) | collective-permute-done | bytes 131104 | tf_op jit(solution)/shard_map/ppermute | solution.py:228
  72.4 0.7 add.7
  73.0 0.0 collective-permute-done.other
  73.0 1.0 %last.1 = f32[2,8,2,2,32,128]{5,4,3,2,1,0:T(8,128)} custom-call(s32[1]{0:T(128)} %bitcast.place, f32[2,8,2,32,128]{4,3,2,1,0:T(8,128)S(1)} %get-tuple-element.10.mine, f32[2,8,2,32,128]{4,3,2,1,0:T(8,128)S(1)} %collective-permute-done.other), custom_call_target="tpu_custom_call" | custom-call | tf_op jit(solution)/shard_map/last/pallas_call | solution.py:220
Async XLA Ops:
  64.5 8.5 %collective-permute-start = (f32[2,8,2,32,128]{4,3,2,1,0:T(8,128)S(1)}, f32[2,8,2,32,128]{4,3,2,1,0:T(8,128)S(1)}, u32[]{:S(2)}, u32[]{:S(2)}) collective-permute-start(f32[2,8,2,32,128]{4,3,2,1,0:T(8,128)S(1)} %get-tuple-element.11), channel_id=1, source_target_pairs={{0,32},{32,0},{1,33},{33,1},{2,34},{34,2},{3,35},{35,3},{4,36},{36... | collective-permute-start | bytes 1572872 | tf_op jit(solution)/shard_map/ppermute | solution.py:219
  65.9 6.5 %collective-permute-start.1 = (f32[8,32,128]{2,1,0:T(8,128)S(1)}, f32[8,32,128]{2,1,0:T(8,128)S(1)}, u32[]{:S(2)}, u32[]{:S(2)}) collective-permute-start(f32[8,32,128]{2,1,0:T(8,128)S(1)} %get-tuple-element.13), channel_id=1, source_target_pairs={{0,64},{64,0},{1,65},{65,1},{2,66},{66,2},{3,67},{67,3},{4,68},{68... | collective-permute-start | bytes 393224 | tf_op jit(solution)/shard_map/ppermute | solution.py:228

commit v7 on v6

--- a/solution.py
+++ b/solution.py
@@ -131,11 +131,27 @@
                 out[r // 8 * 64 + r % 8 * 8 + low, c] = tile
 
 
-def third_kernel(place, got, mine, away, keep, send, held, state):
+def third_kernel(place, got, send, held, state):
+    side = jnp.full((8, 128), (2 * (place[0] >> 1) - 1).astype(F32))
     for r in range(16):
         for c in range(2):
             for b, tile in enumerate(walsh([got[b * 16 + r, c] for b in range(8)])):
                 held[b * 16 + r, c] = tile
+    for b in range(8):
+        chance = [0.0] * 4
+        for c in range(2):
+            low = [held[b * 16 + r, c] + side * held[b * 16 + 8 + r, c] for r in range(8)]
+            for r, tile in enumerate(walsh(low)):
+                state[b * 2 + c, pl.ds(r, 8, stride=8), :] = tile
+            for half in range(2):
+                rows = [mid * 16 + half * 8 for mid in range(4)]
+                for mid, u in enumerate(walsh([state[b * 2 + c, r : r + 8, :] for r in rows])):
+                    chance[mid] = chance[mid] + u * u
+        for mid in range(4):
+            send[b, mid * 8 : mid * 8 + 8, :] = chance[mid] * 0.25
+
+
+def fourth_kernel(place, held, mine, away, keep, state):
     core = (place[0] & 1) == 0
     far = (place[0] >> 1) == 0
     for b in range(8):
@@ -156,7 +172,6 @@
             u = (chance[mid] + chance[8 + mid]) * 0.25
             v = (chance[4 + mid] + chance[12 + mid]) * 0.25
             keep[b, mid * 8 : mid * 8 + 8, :] = jnp.where(far, u, v)
-            send[b, mid * 8 : mid * 8 + 8, :] = jnp.where(far, v, u)
 
 
 def last_kernel(place, mine, other, out, done):
@@ -208,14 +223,23 @@
     )(near(values.reshape(128, 3, 8, 128)), diagonal_angles)
     values = lax.all_to_all(values.reshape(128, 16, 128), ORDER, 0, 0, tiled=True)
     place = bank.reshape(1)
-    mine, away, keep, send = pl.pallas_call(
+    send, held = pl.pallas_call(
         third_kernel,
-        out_shape=(here(2, 8, 2, 32, 128), here(2, 8, 2, 32, 128), here(8, 32, 128), here(8, 32, 128)),
+        out_shape=(here(8, 32, 128), here(128, 2, 8, 128)),
         in_specs=[SMEM, VMEM],
-        out_specs=(VMEM,) * 4,
-        scratch_shapes=[here(128, 2, 8, 128), here(16, 128, 128)],
+        out_specs=(VMEM, VMEM),
+        scratch_shapes=[here(16, 64, 128)],
         name="third",
     )(place, near(values.reshape(128, 2, 8, 128)))
+    sent = lax.ppermute(send, "x_hi", [(0, 1), (1, 0)])
+    mine, away, keep = pl.pallas_call(
+        fourth_kernel,
+        out_shape=(here(2, 8, 2, 32, 128), here(2, 8, 2, 32, 128), here(8, 32, 128)),
+        in_specs=[SMEM, VMEM],
+        out_specs=(VMEM,) * 3,
+        scratch_shapes=[here(16, 128, 128)],
+        name="fourth",
+    )(place, near(held))
     other = lax.ppermute(away, "core", [(0, 1), (1, 0)])
     final = pl.pallas_call(
         last_kernel,
@@ -225,7 +249,6 @@
         scratch_shapes=[pltpu.SemaphoreType.DMA((2, 2))],
         name="last",
     )(place, near(mine), near(other))
-    sent = lax.ppermute(send, "x_hi", [(0, 1), (1, 0)])
     marginal = keep + sent
     return final.reshape(2, 8, 128, 128), marginal
 

time: 74.3 us -> 74.5 us (level)
  no operation moved by 1% of the time
where the time goes in v7:
time: 74.5 us; the launch traced here: 74.2 us
  blocking collectives  58 us (78%)
  Pallas kernels  7.12 us (10%)
  waiting for transfers between devices  5.62 us (8%)
  starting transfers between devices  2.21 us (3%)
    all_to_all x1, blocking collectives, shards(): lax.all_to_all(values.reshape(128, 24, 128), ORDER, 0, 0, tiled=True)  34.2 us
    all_to_all x1, blocking collectives, shards(): lax.all_to_all(values.reshape(128, 16, 128), ORDER, 0, 0, tiled=True)  23.8 us
    ppermute x1, waiting for transfers between devices, shards(): sent = lax.ppermute(send, 'x_hi', [(0, 1), (1, 0)])  5.62 us
    pallas_call x1, Pallas kernels, shards(): pl.pallas_call(first_kernel, out_shape=here(128, 3, 8, 128), in_specs=[HB...  3.26 us
    pallas_call x1, Pallas kernels, shards(): pl.pallas_call(second_kernel, out_shape=here(128, 2, 8, 128), in_specs=[V...  2.09 us
  transfers between devices with their start and end apart: 2, of which 1 were waited for; matrix products, arithmetic and copies ran while one was open for 1% of the time, Pallas kernels for 0%

profile of v7, /device:TPU:1, one launch (start us, length us, event | category | flops | bytes accessed | tf_op | source)
XLA Modules:
  0.0 74.2 jit_solution(1274230246840835065)
XLA Ops:
  0.6 3.3 %first.1 = f32[128,3,8,128]{3,2,1,0:T(8,128)S(1)} custom-call(f32[2,8,128,128]{3,2,1,0:T(8,128)} %amp.1, f32[8,128,128]{2,1,0:T(8,128)} %ener.1, f32[2,128]{1,0:T(2,128)} %angle.1), custom_call_target="tpu_custom_call" | custom-call | tf_op jit(solution)/shard_map/first/pallas_call | solution.py:207
  3.9 34.2 %all_to_all.10 = f32[128,24,128]{2,1,0:T(8,128)S(1)} all-to-all(f32[128,24,128]{2,1,0:T(8,128)S(1)} %bitcast.7), channel_id=1, replica_groups=mesh['x_hi'=2,'core'=2,'z'=4,'y'=4,'x_lo'=2] {'core','y','x_hi','x_lo','z'}, dimensions={0} | all-to-all | bytes 3145728 | tf_op jit(solution)/shard_map/all_to_all | solution.py:215
  38.1 2.1 %second.1 = f32[128,2,8,128]{3,2,1,0:T(8,128)S(1)} custom-call(f32[128,3,8,128]{3,2,1,0:T(8,128)S(1)} %bitcast.6, f32[2,128]{1,0:T(2,128)} %angle.1), custom_call_target="tpu_custom_call" | custom-call | tf_op jit(solution)/shard_map/second/pallas_call | solution.py:216
  40.2 23.8 %all_to_all.11 = f32[128,16,128]{2,1,0:T(8,128)S(1)} all-to-all(f32[128,16,128]{2,1,0:T(8,128)S(1)} %bitcast.8), channel_id=1, replica_groups=mesh['x_hi'=2,'core'=2,'z'=4,'y'=4,'x_lo'=2] {'core','y','x_hi','x_lo','z'}, dimensions={0} | all-to-all | bytes 2097152 | tf_op jit(solution)/shard_map/all_to_all | solution.py:224
  64.0 0.3 third.1
  64.3 0.5 fourth.1
  64.7 1.4 %collective-permute-start = (f32[2,8,2,32,128]{4,3,2,1,0:T(8,128)S(1)}, f32[2,8,2,32,128]{4,3,2,1,0:T(8,128)S(1)}, u32[]{:S(2)}, u32[]{:S(2)}) collective-permute-start(f32[2,8,2,32,128]{4,3,2,1,0:T(8,128)S(1)} %get-tuple-element.13), channel_id=1, source_target_pairs={{0,32},{32,0},{1,33},{33,1},{2,34},{34,2},{3,35},{35,3},{4,36},{36... | collective-permute-start | bytes 1572872 | tf_op jit(solution)/shard_map/ppermute | solution.py:243
  66.1 0.8 %collective-permute-start.1 = (f32[8,32,128]{2,1,0:T(8,128)S(1)}, f32[8,32,128]{2,1,0:T(8,128)S(1)}, u32[]{:S(2)}, u32[]{:S(2)}) collective-permute-start(f32[8,32,128]{2,1,0:T(8,128)S(1)} %get-tuple-element.15), channel_id=1, source_target_pairs={{0,64},{64,0},{1,65},{65,1},{2,66},{66,2},{3,67},{67,3},{4,68},{68... | collective-permute-start | bytes 393224 | tf_op jit(solution)/shard_map/ppermute | solution.py:234
  66.9 5.6 %collective-permute-done.1 = f32[8,32,128]{2,1,0:T(8,128)S(1)} collective-permute-done((f32[8,32,128]{2,1,0:T(8,128)S(1)}, f32[8,32,128]{2,1,0:T(8,128)S(1)}, u32[]{:S(2)}, u32[]{:S(2)}) %collective-permute-start.1) | collective-permute-done | bytes 131104 | tf_op jit(solution)/shard_map/ppermute | solution.py:234
  72.6 0.7 add.7
  73.2 0.0 collective-permute-done.other
  73.2 1.0 %last.1 = f32[2,8,2,2,32,128]{5,4,3,2,1,0:T(8,128)} custom-call(s32[1]{0:T(128)} %bitcast.place, f32[2,8,2,32,128]{4,3,2,1,0:T(8,128)S(1)} %get-tuple-element.12.mine, f32[2,8,2,32,128]{4,3,2,1,0:T(8,128)S(1)} %collective-permute-done.other), custom_call_target="tpu_custom_call" | custom-call | tf_op jit(solution)/shard_map/last/pallas_call | solution.py:244
Async XLA Ops:
  64.7 8.5 %collective-permute-start = (f32[2,8,2,32,128]{4,3,2,1,0:T(8,128)S(1)}, f32[2,8,2,32,128]{4,3,2,1,0:T(8,128)S(1)}, u32[]{:S(2)}, u32[]{:S(2)}) collective-permute-start(f32[2,8,2,32,128]{4,3,2,1,0:T(8,128)S(1)} %get-tuple-element.13), channel_id=1, source_target_pairs={{0,32},{32,0},{1,33},{33,1},{2,34},{34,2},{3,35},{35,3},{4,36},{36... | collective-permute-start | bytes 1572872 | tf_op jit(solution)/shard_map/ppermute | solution.py:243
  66.1 6.5 %collective-permute-start.1 = (f32[8,32,128]{2,1,0:T(8,128)S(1)}, f32[8,32,128]{2,1,0:T(8,128)S(1)}, u32[]{:S(2)}, u32[]{:S(2)}) collective-permute-start(f32[8,32,128]{2,1,0:T(8,128)S(1)} %get-tuple-element.15), channel_id=1, source_target_pairs={{0,64},{64,0},{1,65},{65,1},{2,66},{66,2},{3,67},{67,3},{4,68},{68... | collective-permute-start | bytes 393224 | tf_op jit(solution)/shard_map/ppermute | solution.py:234

commit v8 on v7

--- a/solution.py
+++ b/solution.py
@@ -71,7 +71,7 @@
     return [x[r * 8 : r * 8 + 8] for r in range(x.shape[0] // 8)]
 
 
-def first_kernel(amp, ener, angle, out, held, state, arrived):
+def first_kernel(amp, ener, given, out, angle, held, state, arrived, known):
     def copies(b):
         return [
             pltpu.make_async_copy(amp.at[0, b], held.at[b, 0], arrived.at[b, 0]),
@@ -79,11 +79,14 @@
             pltpu.make_async_copy(ener.at[b], held.at[b, 2], arrived.at[b, 2]),
         ]
 
+    angles = pltpu.make_async_copy(given, angle, known)
+    angles.start()
     for b in range(8):
         for copy in copies(b):
             copy.start()
     starts = {sum(GROUPS[:i]): size for i, size in enumerate(GROUPS)}
     sign = signs()
+    angles.wait()
     a = angle[0:1, :] * 0.5
     for b in range(8):
         if b in starts:
@@ -204,12 +207,17 @@
 
 def shards(amplitudes, energies, diagonal_angles):
     diagonal_angles, bank = lax.optimization_barrier((diagonal_angles, lax.axis_index(BANK)))
-    values = pl.pallas_call(
+    values, angles = pl.pallas_call(
         first_kernel,
-        out_shape=here(128, 3, 8, 128),
-        in_specs=[HBM, HBM, VMEM],
-        out_specs=VMEM,
-        scratch_shapes=[here(8, 3, 128, 128), here(16, 128, 128), pltpu.SemaphoreType.DMA((8, 3))],
+        out_shape=(here(128, 3, 8, 128), here(2, 128)),
+        in_specs=[HBM] * 3,
+        out_specs=(VMEM, VMEM),
+        scratch_shapes=[
+            here(8, 3, 128, 128),
+            here(16, 128, 128),
+            pltpu.SemaphoreType.DMA((8, 3)),
+            pltpu.SemaphoreType.DMA,
+        ],
         name="first",
     )(amplitudes, energies, diagonal_angles)
     values = lax.all_to_all(values.reshape(128, 24, 128), ORDER, 0, 0, tiled=True)
@@ -220,7 +228,7 @@
         out_specs=VMEM,
         scratch_shapes=[here(128, 2, 8, 128), here(2, 64, 16, 128)],
         name="second",
-    )(near(values.reshape(128, 3, 8, 128)), diagonal_angles)
+    )(near(values.reshape(128, 3, 8, 128)), near(angles))
     values = lax.all_to_all(values.reshape(128, 16, 128), ORDER, 0, 0, tiled=True)
     place = bank.reshape(1)
     send, held = pl.pallas_call(

time: 74.5 us -> 73.3 us (0.984)
  Pallas kernels: 7.12 us -> 6.01 us
where the time goes in v8:
time: 73.3 us; the launch traced here: 73.1 us
  blocking collectives  58 us (79%)
  Pallas kernels  6.01 us (8%)
  waiting for transfers between devices  5.62 us (8%)
  starting transfers between devices  2.21 us (3%)
    all_to_all x1, blocking collectives, shards(): lax.all_to_all(values.reshape(128, 24, 128), ORDER, 0, 0, tiled=True)  34.2 us
    all_to_all x1, blocking collectives, shards(): lax.all_to_all(values.reshape(128, 16, 128), ORDER, 0, 0, tiled=True)  23.8 us
    ppermute x1, waiting for transfers between devices, shards(): sent = lax.ppermute(send, 'x_hi', [(0, 1), (1, 0)])  5.62 us
    pallas_call x1, Pallas kernels, shards(): pl.pallas_call(first_kernel, out_shape=(here(128, 3, 8, 128), here(2, 128...  2.82 us
  transfers between devices with their start and end apart: 2, of which 1 were waited for; matrix products, arithmetic and copies ran while one was open for 1% of the time, Pallas kernels for 0%

profile of v8, /device:TPU:1, one launch (start us, length us, event | category | flops | bytes accessed | tf_op | source)
XLA Modules:
  0.0 73.1 jit_solution(6093456706403109463)
XLA Ops:
  0.6 2.8 %first.1 = (f32[128,3,8,128]{3,2,1,0:T(8,128)S(1)}, f32[2,128]{1,0:T(2,128)S(1)}) custom-call(f32[2,8,128,128]{3,2,1,0:T(8,128)} %amp.1, f32[8,128,128]{2,1,0:T(8,128)} %ener.1, f32[2,128]{1,0:T(2,128)} %given), custom_call_target="tpu_custom_call" | custom-call | tf_op jit(solution)/shard_map/first/pallas_call | solution.py:210
  3.5 34.2 %all_to_all.10 = f32[128,24,128]{2,1,0:T(8,128)S(1)} all-to-all(f32[128,24,128]{2,1,0:T(8,128)S(1)} %bitcast.9), channel_id=1, replica_groups=mesh['x_hi'=2,'core'=2,'z'=4,'y'=4,'x_lo'=2] {'core','y','x_hi','x_lo','z'}, dimensions={0} | all-to-all | bytes 3145728 | tf_op jit(solution)/shard_map/all_to_all | solution.py:223
  37.7 1.4 %second.1 = f32[128,2,8,128]{3,2,1,0:T(8,128)S(1)} custom-call(f32[128,3,8,128]{3,2,1,0:T(8,128)S(1)} %bitcast.6, f32[2,128]{1,0:T(2,128)S(1)} %get-tuple-element.14.angle), custom_call_target="tpu_custom_call" | custom-call | tf_op jit(solution)/shard_map/second/pallas_call | solution.py:224
  39.1 23.8 %all_to_all.11 = f32[128,16,128]{2,1,0:T(8,128)S(1)} all-to-all(f32[128,16,128]{2,1,0:T(8,128)S(1)} %bitcast.7), channel_id=1, replica_groups=mesh['x_hi'=2,'core'=2,'z'=4,'y'=4,'x_lo'=2] {'core','y','x_hi','x_lo','z'}, dimensions={0} | all-to-all | bytes 2097152 | tf_op jit(solution)/shard_map/all_to_all | solution.py:232
  62.9 0.3 third.1
  63.2 0.5 fourth.1
  63.6 1.4 %collective-permute-start = (f32[2,8,2,32,128]{4,3,2,1,0:T(8,128)S(1)}, f32[2,8,2,32,128]{4,3,2,1,0:T(8,128)S(1)}, u32[]{:S(2)}, u32[]{:S(2)}) collective-permute-start(f32[2,8,2,32,128]{4,3,2,1,0:T(8,128)S(1)} %get-tuple-element.17), channel_id=1, source_target_pairs={{0,32},{32,0},{1,33},{33,1},{2,34},{34,2},{3,35},{35,3},{4,36},{36... | collective-permute-start | bytes 1572872 | tf_op jit(solution)/shard_map/ppermute | solution.py:251
  65.0 0.8 %collective-permute-start.1 = (f32[8,32,128]{2,1,0:T(8,128)S(1)}, f32[8,32,128]{2,1,0:T(8,128)S(1)}, u32[]{:S(2)}, u32[]{:S(2)}) collective-permute-start(f32[8,32,128]{2,1,0:T(8,128)S(1)} %get-tuple-element.19), channel_id=1, source_target_pairs={{0,64},{64,0},{1,65},{65,1},{2,66},{66,2},{3,67},{67,3},{4,68},{68... | collective-permute-start | bytes 393224 | tf_op jit(solution)/shard_map/ppermute | solution.py:242
  65.8 5.6 %collective-permute-done.1 = f32[8,32,128]{2,1,0:T(8,128)S(1)} collective-permute-done((f32[8,32,128]{2,1,0:T(8,128)S(1)}, f32[8,32,128]{2,1,0:T(8,128)S(1)}, u32[]{:S(2)}, u32[]{:S(2)}) %collective-permute-start.1) | collective-permute-done | bytes 131104 | tf_op jit(solution)/shard_map/ppermute | solution.py:242
  71.5 0.7 add.7
  72.1 0.0 collective-permute-done.other
  72.1 1.0 %last.1 = f32[2,8,2,2,32,128]{5,4,3,2,1,0:T(8,128)} custom-call(s32[1]{0:T(128)} %bitcast.place, f32[2,8,2,32,128]{4,3,2,1,0:T(8,128)S(1)} %get-tuple-element.16.mine, f32[2,8,2,32,128]{4,3,2,1,0:T(8,128)S(1)} %collective-permute-done.other), custom_call_target="tpu_custom_call" | custom-call | tf_op jit(solution)/shard_map/last/pallas_call | solution.py:252
Async XLA Ops:
  63.6 8.5 %collective-permute-start = (f32[2,8,2,32,128]{4,3,2,1,0:T(8,128)S(1)}, f32[2,8,2,32,128]{4,3,2,1,0:T(8,128)S(1)}, u32[]{:S(2)}, u32[]{:S(2)}) collective-permute-start(f32[2,8,2,32,128]{4,3,2,1,0:T(8,128)S(1)} %get-tuple-element.17), channel_id=1, source_target_pairs={{0,32},{32,0},{1,33},{33,1},{2,34},{34,2},{3,35},{35,3},{4,36},{36... | collective-permute-start | bytes 1572872 | tf_op jit(solution)/shard_map/ppermute | solution.py:251
  65.0 6.5 %collective-permute-start.1 = (f32[8,32,128]{2,1,0:T(8,128)S(1)}, f32[8,32,128]{2,1,0:T(8,128)S(1)}, u32[]{:S(2)}, u32[]{:S(2)}) collective-permute-start(f32[8,32,128]{2,1,0:T(8,128)S(1)} %get-tuple-element.19), channel_id=1, source_target_pairs={{0,64},{64,0},{1,65},{65,1},{2,66},{66,2},{3,67},{67,3},{4,68},{68... | collective-permute-start | bytes 393224 | tf_op jit(solution)/shard_map/ppermute | solution.py:242

commit v9 on v8

--- a/solution.py
+++ b/solution.py
@@ -9,7 +9,7 @@
 
 F32 = jnp.float32
 BF16 = jnp.bfloat16
-GROUPS = (2, 3, 3)
+GROUPS = (3, 5)
 SCALE = 2.0**-13
 
 
@@ -21,7 +21,7 @@
     return [float(c) for c in np.linalg.lstsq(powers / scale, 2 * np.sin(x), rcond=None)[0] / scale]
 
 
-SIN = fit(6, 1.4)
+SIN = fit(5, 1.3)
 
 
 def turned(re, im, half):
@@ -51,20 +51,21 @@
     both = lax.broadcasted_iota(jnp.int32, (128, 128), 0) & lax.broadcasted_iota(jnp.int32, (128, 128), 1)
     for shift in (4, 2, 1):
         both = both ^ (both >> shift)
-    return ((1 - 2 * (both & 1)).astype(F32) * SCALE).astype(BF16)
+    sign = ((1 - 2 * (both & 1)).astype(F32) * SCALE).astype(BF16)
+    return jnp.concatenate([jnp.concatenate([sign, sign], 1), jnp.concatenate([sign, -sign], 1)], 0)
 
 
 PIECES = 2
 
 
-def mixed(re, im, sign):
-    rest = jnp.concatenate([re, im], 0)
+def mixed(part, sign):
+    rest = jnp.concatenate([part[:64], part[64:]], 1)
     pieces = []
     for _ in range(PIECES):
         pieces.append(rest.astype(BF16))
         rest = rest - pieces[-1].astype(F32)
     both = jnp.dot(jnp.concatenate(pieces, 1), jnp.concatenate([sign] * PIECES, 0), preferred_element_type=F32)
-    return both[:128], both[128:]
+    return walsh(tiles(both[:, :128])) + walsh(tiles(both[:, 128:]))
 
 
 def tiles(x):
@@ -94,8 +95,8 @@
                 for copy in copies(ready):
                     copy.wait()
         re, im = turned(held[b, 0], held[b, 1], a * held[b, 2])
-        for c, part in enumerate(mixed(re, im, sign)):
-            for r, tile in enumerate(walsh(tiles(part))):
+        for c, part in enumerate((re, im)):
+            for r, tile in enumerate(mixed(part, sign)):
                 state[b * 2 + c, r * 8 : r * 8 + 8, :] = tile
         for top in range(2):
             for low in range(8):
@@ -124,8 +125,8 @@
         im = jnp.concatenate(walsh([held[row, 1] for row in rows]), 0)
         e = jnp.concatenate([got[row, 2] for row in rows], 0)
         re, im = turned(re, im, a * e)
-        for c, part in enumerate(mixed(re, im, sign)):
-            for r, tile in enumerate(walsh(tiles(part))):
+        for c, part in enumerate((re, im)):
+            for r, tile in enumerate(mixed(part, sign)):
                 state[c, high * 8 + r % 8, pl.ds(r // 8, 8, stride=2), :] = tile
     for low in range(8):
         for c in range(2):

time: 73.3 us -> 73.2 us (level)
  no operation moved by 1% of the time
where the time goes in v9:
time: 73.2 us; the launch traced here: 73 us
  blocking collectives  58 us (79%)
  Pallas kernels  5.9 us (8%)
  waiting for transfers between devices  5.62 us (8%)
  starting transfers between devices  2.21 us (3%)
    all_to_all x1, blocking collectives, shards(): lax.all_to_all(values.reshape(128, 24, 128), ORDER, 0, 0, tiled=True)  34.2 us
    all_to_all x1, blocking collectives, shards(): lax.all_to_all(values.reshape(128, 16, 128), ORDER, 0, 0, tiled=True)  23.8 us
    ppermute x1, waiting for transfers between devices, shards(): sent = lax.ppermute(send, 'x_hi', [(0, 1), (1, 0)])  5.62 us
    pallas_call x1, Pallas kernels, shards(): pl.pallas_call(first_kernel, out_shape=(here(128, 3, 8, 128), here(2, 128...  2.77 us
  transfers between devices with their start and end apart: 2, of which 1 were waited for; matrix products, arithmetic and copies ran while one was open for 1% of the time, Pallas kernels for 0%

profile of v9, /device:TPU:1, one launch (start us, length us, event | category | flops | bytes accessed | tf_op | source)
XLA Modules:
  0.0 73.0 jit_solution(14538885230863566829)
XLA Ops:
  0.6 2.8 %first.1 = (f32[128,3,8,128]{3,2,1,0:T(8,128)S(1)}, f32[2,128]{1,0:T(2,128)S(1)}) custom-call(f32[2,8,128,128]{3,2,1,0:T(8,128)} %amp.1, f32[8,128,128]{2,1,0:T(8,128)} %ener.1, f32[2,128]{1,0:T(2,128)} %given), custom_call_target="tpu_custom_call" | custom-call | tf_op jit(solution)/shard_map/first/pallas_call | solution.py:211
  3.4 34.2 %all_to_all.10 = f32[128,24,128]{2,1,0:T(8,128)S(1)} all-to-all(f32[128,24,128]{2,1,0:T(8,128)S(1)} %bitcast.9), channel_id=1, replica_groups=mesh['x_hi'=2,'core'=2,'z'=4,'y'=4,'x_lo'=2] {'core','y','x_hi','x_lo','z'}, dimensions={0} | all-to-all | bytes 3145728 | tf_op jit(solution)/shard_map/all_to_all | solution.py:224
  37.6 1.4 %second.1 = f32[128,2,8,128]{3,2,1,0:T(8,128)S(1)} custom-call(f32[128,3,8,128]{3,2,1,0:T(8,128)S(1)} %bitcast.6, f32[2,128]{1,0:T(2,128)S(1)} %get-tuple-element.14.angle), custom_call_target="tpu_custom_call" | custom-call | tf_op jit(solution)/shard_map/second/pallas_call | solution.py:225
  39.0 23.8 %all_to_all.11 = f32[128,16,128]{2,1,0:T(8,128)S(1)} all-to-all(f32[128,16,128]{2,1,0:T(8,128)S(1)} %bitcast.7), channel_id=1, replica_groups=mesh['x_hi'=2,'core'=2,'z'=4,'y'=4,'x_lo'=2] {'core','y','x_hi','x_lo','z'}, dimensions={0} | all-to-all | bytes 2097152 | tf_op jit(solution)/shard_map/all_to_all | solution.py:233
  62.7 0.3 third.1
  63.1 0.5 fourth.1
  63.5 1.4 %collective-permute-start = (f32[2,8,2,32,128]{4,3,2,1,0:T(8,128)S(1)}, f32[2,8,2,32,128]{4,3,2,1,0:T(8,128)S(1)}, u32[]{:S(2)}, u32[]{:S(2)}) collective-permute-start(f32[2,8,2,32,128]{4,3,2,1,0:T(8,128)S(1)} %get-tuple-element.17), channel_id=1, source_target_pairs={{0,32},{32,0},{1,33},{33,1},{2,34},{34,2},{3,35},{35,3},{4,36},{36... | collective-permute-start | bytes 1572872 | tf_op jit(solution)/shard_map/ppermute | solution.py:252
  64.9 0.8 %collective-permute-start.1 = (f32[8,32,128]{2,1,0:T(8,128)S(1)}, f32[8,32,128]{2,1,0:T(8,128)S(1)}, u32[]{:S(2)}, u32[]{:S(2)}) collective-permute-start(f32[8,32,128]{2,1,0:T(8,128)S(1)} %get-tuple-element.19), channel_id=1, source_target_pairs={{0,64},{64,0},{1,65},{65,1},{2,66},{66,2},{3,67},{67,3},{4,68},{68... | collective-permute-start | bytes 393224 | tf_op jit(solution)/shard_map/ppermute | solution.py:243
  65.7 5.6 %collective-permute-done.1 = f32[8,32,128]{2,1,0:T(8,128)S(1)} collective-permute-done((f32[8,32,128]{2,1,0:T(8,128)S(1)}, f32[8,32,128]{2,1,0:T(8,128)S(1)}, u32[]{:S(2)}, u32[]{:S(2)}) %collective-permute-start.1) | collective-permute-done | bytes 131104 | tf_op jit(solution)/shard_map/ppermute | solution.py:243
  71.4 0.7 add.7
  72.0 0.0 collective-permute-done.other
  72.0 1.0 %last.1 = f32[2,8,2,2,32,128]{5,4,3,2,1,0:T(8,128)} custom-call(s32[1]{0:T(128)} %bitcast.place, f32[2,8,2,32,128]{4,3,2,1,0:T(8,128)S(1)} %get-tuple-element.16.mine, f32[2,8,2,32,128]{4,3,2,1,0:T(8,128)S(1)} %collective-permute-done.other), custom_call_target="tpu_custom_call" | custom-call | tf_op jit(solution)/shard_map/last/pallas_call | solution.py:253
Async XLA Ops:
  63.5 8.5 %collective-permute-start = (f32[2,8,2,32,128]{4,3,2,1,0:T(8,128)S(1)}, f32[2,8,2,32,128]{4,3,2,1,0:T(8,128)S(1)}, u32[]{:S(2)}, u32[]{:S(2)}) collective-permute-start(f32[2,8,2,32,128]{4,3,2,1,0:T(8,128)S(1)} %get-tuple-element.17), channel_id=1, source_target_pairs={{0,32},{32,0},{1,33},{33,1},{2,34},{34,2},{3,35},{35,3},{4,36},{36... | collective-permute-start | bytes 1572872 | tf_op jit(solution)/shard_map/ppermute | solution.py:252
  64.9 6.5 %collective-permute-start.1 = (f32[8,32,128]{2,1,0:T(8,128)S(1)}, f32[8,32,128]{2,1,0:T(8,128)S(1)}, u32[]{:S(2)}, u32[]{:S(2)}) collective-permute-start(f32[8,32,128]{2,1,0:T(8,128)S(1)} %get-tuple-element.19), channel_id=1, source_target_pairs={{0,64},{64,0},{1,65},{65,1},{2,66},{66,2},{3,67},{67,3},{4,68},{68... | collective-permute-start | bytes 393224 | tf_op jit(solution)/shard_map/ppermute | solution.py:243

commit v10 on v9

--- a/solution.py
+++ b/solution.py
@@ -137,14 +137,15 @@
 
 def third_kernel(place, got, send, held, state):
     side = jnp.full((8, 128), (2 * (place[0] >> 1) - 1).astype(F32))
-    for r in range(16):
-        for c in range(2):
-            for b, tile in enumerate(walsh([got[b * 16 + r, c] for b in range(8)])):
-                held[b * 16 + r, c] = tile
+    for r in range(8):
+        for c in range(2):
+            kept = [got[b * 16 + r, c] + side * got[b * 16 + 8 + r, c] for b in range(8)]
+            for b, tile in enumerate(walsh(kept)):
+                held[b * 8 + r, c] = tile
     for b in range(8):
         chance = [0.0] * 4
         for c in range(2):
-            low = [held[b * 16 + r, c] + side * held[b * 16 + 8 + r, c] for r in range(8)]
+            low = [held[b * 8 + r, c] for r in range(8)]
             for r, tile in enumerate(walsh(low)):
                 state[b * 2 + c, pl.ds(r, 8, stride=8), :] = tile
             for half in range(2):
@@ -155,7 +156,11 @@
             send[b, mid * 8 : mid * 8 + 8, :] = chance[mid] * 0.25
 
 
-def fourth_kernel(place, held, mine, away, keep, state):
+def fourth_kernel(place, got, mine, away, keep, held, state):
+    for r in range(16):
+        for c in range(2):
+            for b, tile in enumerate(walsh([got[b * 16 + r, c] for b in range(8)])):
+                held[b * 16 + r, c] = tile
     core = (place[0] & 1) == 0
     far = (place[0] >> 1) == 0
     for b in range(8):
@@ -203,7 +208,7 @@
 HBM = pl.BlockSpec(memory_space=pltpu.HBM)
 BANK = ("x_hi", "core")
 LANE = ("z", "y", "x_lo")
-ORDER = ("core", "y", "x_hi", "x_lo", "z")
+ORDER = ("core", "x_hi", "x_lo", "y", "z")
 
 
 def shards(amplitudes, energies, diagonal_angles):
@@ -232,23 +237,24 @@
     )(near(values.reshape(128, 3, 8, 128)), near(angles))
     values = lax.all_to_all(values.reshape(128, 16, 128), ORDER, 0, 0, tiled=True)
     place = bank.reshape(1)
-    send, held = pl.pallas_call(
+    values = near(values.reshape(128, 2, 8, 128))
+    send = pl.pallas_call(
         third_kernel,
-        out_shape=(here(8, 32, 128), here(128, 2, 8, 128)),
+        out_shape=here(8, 32, 128),
         in_specs=[SMEM, VMEM],
-        out_specs=(VMEM, VMEM),
-        scratch_shapes=[here(16, 64, 128)],
+        out_specs=VMEM,
+        scratch_shapes=[here(64, 2, 8, 128), here(16, 64, 128)],
         name="third",
-    )(place, near(values.reshape(128, 2, 8, 128)))
+    )(place, values)
     sent = lax.ppermute(send, "x_hi", [(0, 1), (1, 0)])
     mine, away, keep = pl.pallas_call(
         fourth_kernel,
         out_shape=(here(2, 8, 2, 32, 128), here(2, 8, 2, 32, 128), here(8, 32, 128)),
         in_specs=[SMEM, VMEM],
         out_specs=(VMEM,) * 3,
-        scratch_shapes=[here(16, 128, 128)],
+        scratch_shapes=[here(128, 2, 8, 128), here(16, 128, 128)],
         name="fourth",
-    )(place, near(held))
+    )(place, values)
     other = lax.ppermute(away, "core", [(0, 1), (1, 0)])
     final = pl.pallas_call(
         last_kernel,

time: 73.2 us -> 73.4 us (level)
  no operation moved by 1% of the time
where the time goes in v10:
time: 73.4 us; the launch traced here: 73.2 us
  blocking collectives  57.9 us (79%)
  Pallas kernels  5.95 us (8%)
  waiting for transfers between devices  5.82 us (8%)
  starting transfers between devices  2.19 us (3%)
    all_to_all x1, blocking collectives, shards(): lax.all_to_all(values.reshape(128, 24, 128), ORDER, 0, 0, tiled=True)  34.1 us
    all_to_all x1, blocking collectives, shards(): lax.all_to_all(values.reshape(128, 16, 128), ORDER, 0, 0, tiled=True)  23.7 us
    ppermute x1, waiting for transfers between devices, shards(): sent = lax.ppermute(send, 'x_hi', [(0, 1), (1, 0)])  5.82 us
    pallas_call x1, Pallas kernels, shards(): pl.pallas_call(first_kernel, out_shape=(here(128, 3, 8, 128), here(2, 128...  2.77 us
  transfers between devices with their start and end apart: 2, of which 1 were waited for; matrix products, arithmetic and copies ran while one was open for 1% of the time, Pallas kernels for 0%

profile of v10, /device:TPU:1, one launch (start us, length us, event | category | flops | bytes accessed | tf_op | source)
XLA Modules:
  0.0 73.2 jit_solution(5570551924062504704)
XLA Ops:
  0.6 2.8 %first.1 = (f32[128,3,8,128]{3,2,1,0:T(8,128)S(1)}, f32[2,128]{1,0:T(2,128)S(1)}) custom-call(f32[2,8,128,128]{3,2,1,0:T(8,128)} %amp.1, f32[8,128,128]{2,1,0:T(8,128)} %ener.1, f32[2,128]{1,0:T(2,128)} %given), custom_call_target="tpu_custom_call" | custom-call | tf_op jit(solution)/shard_map/first/pallas_call | solution.py:216
  3.4 34.1 %all_to_all.10 = f32[128,24,128]{2,1,0:T(8,128)S(1)} all-to-all(f32[128,24,128]{2,1,0:T(8,128)S(1)} %bitcast.10), channel_id=1, replica_groups=mesh['x_hi'=2,'core'=2,'z'=4,'y'=4,'x_lo'=2] {'core','x_hi','x_lo','y','z'}, dimensions={0} | all-to-all | bytes 3145728 | tf_op jit(solution)/shard_map/all_to_all | solution.py:229
  37.5 1.4 %second.1 = f32[128,2,8,128]{3,2,1,0:T(8,128)S(1)} custom-call(f32[128,3,8,128]{3,2,1,0:T(8,128)S(1)} %bitcast.8, f32[2,128]{1,0:T(2,128)S(1)} %get-tuple-element.12.angle), custom_call_target="tpu_custom_call" | custom-call | tf_op jit(solution)/shard_map/second/pallas_call | solution.py:230
  38.9 23.7 %all_to_all.11 = f32[128,16,128]{2,1,0:T(8,128)S(1)} all-to-all(f32[128,16,128]{2,1,0:T(8,128)S(1)} %bitcast.9), channel_id=1, replica_groups=mesh['x_hi'=2,'core'=2,'z'=4,'y'=4,'x_lo'=2] {'core','x_hi','x_lo','y','z'}, dimensions={0} | all-to-all | bytes 2097152 | tf_op jit(solution)/shard_map/all_to_all | solution.py:238
  62.7 0.6 fourth.1
  63.2 1.4 %collective-permute-start = (f32[2,8,2,32,128]{4,3,2,1,0:T(8,128)S(1)}, f32[2,8,2,32,128]{4,3,2,1,0:T(8,128)S(1)}, u32[]{:S(2)}, u32[]{:S(2)}) collective-permute-start(f32[2,8,2,32,128]{4,3,2,1,0:T(8,128)S(1)} %get-tuple-element.14), channel_id=1, source_target_pairs={{0,32},{32,0},{1,33},{33,1},{2,34},{34,2},{3,35},{35,3},{4,36},{36... | collective-permute-start | bytes 1572872 | tf_op jit(solution)/shard_map/ppermute | solution.py:258
  64.6 0.3 third.1
  64.9 0.8 %collective-permute-start.1 = (f32[8,32,128]{2,1,0:T(8,128)S(1)}, f32[8,32,128]{2,1,0:T(8,128)S(1)}, u32[]{:S(2)}, u32[]{:S(2)}) collective-permute-start(f32[8,32,128]{2,1,0:T(8,128)S(1)} %third.1), channel_id=1, source_target_pairs={{0,64},{64,0},{1,65},{65,1},{2,66},{66,2},{3,67},{67,3},{4,68},{68... | collective-permute-start | bytes 393224 | tf_op jit(solution)/shard_map/ppermute | solution.py:249
  65.7 5.8 %collective-permute-done.1 = f32[8,32,128]{2,1,0:T(8,128)S(1)} collective-permute-done((f32[8,32,128]{2,1,0:T(8,128)S(1)}, f32[8,32,128]{2,1,0:T(8,128)S(1)}, u32[]{:S(2)}, u32[]{:S(2)}) %collective-permute-start.1) | collective-permute-done | bytes 131104 | tf_op jit(solution)/shard_map/ppermute | solution.py:249
  71.5 0.7 add.7
  72.2 0.0 collective-permute-done.other
  72.2 1.0 %last.1 = f32[2,8,2,2,32,128]{5,4,3,2,1,0:T(8,128)} custom-call(s32[1]{0:T(128)} %bitcast.place, f32[2,8,2,32,128]{4,3,2,1,0:T(8,128)S(1)} %get-tuple-element.13.mine, f32[2,8,2,32,128]{4,3,2,1,0:T(8,128)S(1)} %collective-permute-done.other), custom_call_target="tpu_custom_call" | custom-call | tf_op jit(solution)/shard_map/last/pallas_call | solution.py:259
Async XLA Ops:
  63.2 9.0 %collective-permute-start = (f32[2,8,2,32,128]{4,3,2,1,0:T(8,128)S(1)}, f32[2,8,2,32,128]{4,3,2,1,0:T(8,128)S(1)}, u32[]{:S(2)}, u32[]{:S(2)}) collective-permute-start(f32[2,8,2,32,128]{4,3,2,1,0:T(8,128)S(1)} %get-tuple-element.14), channel_id=1, source_target_pairs={{0,32},{32,0},{1,33},{33,1},{2,34},{34,2},{3,35},{35,3},{4,36},{36... | collective-permute-start | bytes 1572872 | tf_op jit(solution)/shard_map/ppermute | solution.py:258
  64.9 6.6 %collective-permute-start.1 = (f32[8,32,128]{2,1,0:T(8,128)S(1)}, f32[8,32,128]{2,1,0:T(8,128)S(1)}, u32[]{:S(2)}, u32[]{:S(2)}) collective-permute-start(f32[8,32,128]{2,1,0:T(8,128)S(1)} %third.1), channel_id=1, source_target_pairs={{0,64},{64,0},{1,65},{65,1},{2,66},{66,2},{3,67},{67,3},{4,68},{68... | collective-permute-start | bytes 393224 | tf_op jit(solution)/shard_map/ppermute | solution.py:249
